TPU v7x, 256 devices: a whole 4x4x8 slice. The times are simulated.
256 devices in a mesh: dp: 64 (over y, z, core), member: 4 (over x).
Axes of the slice: x: 4, y: 4, z: 8, core: 2. Of those that a mesh axis runs over, the one named last changes fastest.
Arguments:
- features: bfloat16 [32768, 256], P('dp'), may hold values from -6 to 6
- next_features: bfloat16 [32768, 256], P('dp'), may hold values from -6 to 6
- rewards: bfloat16 [32768], P('dp'), may hold values from -6 to 6
- next_logp: bfloat16 [32768], P('dp'), may hold values from -8 to 8
- terminal: int32 [32768], P('dp'), may hold values 0 or 1
- source_ids: int32 [32768], P('dp'), may hold values from 0 to 7
- source_weight: bfloat16 [8], replicated, may hold values from 0.29882812 to 3
- subset: int32 [32768, 2], P('dp'), may hold values from 0 to 7, all different within a row
- destination: int32 [32768], P('dp'), may hold values from 0 to 63, as said below
- critic_w1: float32 [8, 2048, 256], P('member'), may hold values from -0.375 to 0.375
- critic_shift: float32 [8, 2048], P('member'), may hold values from -3 to 3
- critic_head: float32 [8, 2048], P('member'), may hold values from -0.125 to 0.125
- target_w1: bfloat16 [8, 2048, 256], P('member'), may hold values from -0.375 to 0.375
- target_mean: float32 [8, 2048], P('member'), may hold values from -2 to 2
- target_scale: float32 [8, 2048], P('member'), may hold values from 0.5 to 2
- target_shift: float32 [8, 2048], P('member'), may hold values from -3 to 3
- target_head: float32 [8, 2048], P('member'), may hold values from -0.125 to 0.125
Outputs:
- step_w1: float32 [8, 2048, 256], P('member')
- step_shift: float32 [8, 2048], P('member')
- step_head: float32 [8, 2048], P('member')
Inputs may be any that keep to these rules, and one draw needn't show every extreme that they name: `destination`: in the 512 transitions that start on one index of dp, every shard is named at least 512 // 128 times and at most 16 times, and some shard exactly 16 times. `subset`: the entries of a row differ.
All inputs are finite; a program needn't handle non-finite values. No bound on the sum of `terminal` on one device may be relied on, other than what follows from the above.
Results may differ from a plain program's by a relative error of at most 0.003.
The roundings to bfloat16 on the way count: a program that leaves them out, or rounds other values in their place, can miss the bound.
Values may be sent and summed in bfloat16 or wider, within the bound.
A program may use at most 128 MiB of HBM per device.

v0:
```python
import math

import jax
import jax.numpy as jnp
from jax import lax
from jax.sharding import PartitionSpec as P

GAMMA = 0.99
ALPHA = 0.2
EPS = 1e-05


def in_one(arrays, axis):
    ends = [0]
    for a in arrays:
        ends.append(ends[-1] + a.size)
    running = lax.psum(jnp.concatenate([a.ravel() for a in arrays]), axis)
    return tuple((running[b:e].reshape(a.shape) for a, b, e in zip(arrays, ends, ends[1:])))


def sent_to_all(array, axis):
    copies = jnp.broadcast_to(array, (lax.axis_size(axis), *array.shape))
    return lax.all_to_all(copies, axis, split_axis=0, concat_axis=0, tiled=True)


def over_copies(array, axis):
    everything = sent_to_all(array, axis)
    return jnp.sum(everything, axis=0)


def per_device(
    features,
    next_features,
    rewards,
    next_logp,
    terminal,
    source_ids,
    source_weight,
    subset,
    destination,
    critic_w1,
    critic_shift,
    critic_head,
    target_w1,
    target_mean,
    target_scale,
    target_shift,
    target_head,
):
    shards = lax.axis_size("dp")
    members = lax.axis_size("member")
    local_rows = features.shape[0]
    width = features.shape[1]
    local_critics = critic_w1.shape[0]
    total_critics = local_critics * members
    capacity = 2 * local_rows // shards
    slot_total = shards * capacity
    shard_iota = jnp.arange(shards, dtype=jnp.int32)
    picked = (destination[:, None] == shard_iota[None]).astype(jnp.int32)
    earlier = jnp.cumsum(picked, axis=0) - picked
    rank = jnp.sum(earlier * picked, axis=1)
    position = destination * capacity + rank

    def place(values):
        empty = jnp.zeros((slot_total,) + values.shape[1:], values.dtype)
        return empty.at[position].set(values).reshape((shards, capacity) + values.shape[1:])

    source_iota = jnp.arange(source_weight.shape[0], dtype=jnp.int32)
    weight_rows = jnp.sum(
        jnp.where(
            source_ids[:, None] == source_iota[None], source_weight.astype(jnp.float32)[None], 0.0
        ),
        axis=1,
    ).astype(jnp.bfloat16)
    carry_rows = (1 - terminal).astype(jnp.bfloat16)
    pre_act = jnp.einsum(
        "si,cfi->csf", next_features, target_w1, preferred_element_type=jnp.float32
    )
    active = jnp.maximum(
        (pre_act - target_mean[:, None]) * target_scale[:, None] + target_shift[:, None], 0.0
    )
    mine = jnp.sum(active * target_head[:, None], axis=2).T
    everyone = lax.all_gather(mine, "member", axis=1, tiled=True)
    critic_iota = jnp.arange(total_critics, dtype=jnp.int32)
    first = jnp.sum(jnp.where(subset[:, 0][:, None] == critic_iota[None], everyone, 0.0), axis=1)
    second = jnp.sum(jnp.where(subset[:, 1][:, None] == critic_iota[None], everyone, 0.0), axis=1)
    lowest = jnp.minimum(first, second)
    value = rewards.astype(jnp.float32) + GAMMA * carry_rows.astype(jnp.float32) * (
        lowest - ALPHA * next_logp.astype(jnp.float32)
    )
    value = value.astype(jnp.bfloat16)
    received, weight_slots, target_slots = (
        lax.all_to_all(place(features), "dp", split_axis=0, concat_axis=0, tiled=True),
        lax.all_to_all(place(weight_rows), "dp", split_axis=0, concat_axis=0, tiled=True),
        lax.all_to_all(place(value), "dp", split_axis=0, concat_axis=0, tiled=True),
    )
    rows_in = received.reshape(slot_total, width)
    weight = weight_slots.reshape(slot_total).astype(jnp.float32)
    target = target_slots.reshape(slot_total).astype(jnp.float32)
    live = (weight > 0).astype(jnp.float32)
    live_count = jnp.sum(live)
    live_col = live[:, None]

    def critic(params):
        weights, offset, output = params
        pre_act = jnp.dot(
            rows_in, weights.astype(jnp.bfloat16).T, preferred_element_type=jnp.float32
        )
        centred = pre_act - jnp.sum(pre_act * live_col, axis=0, keepdims=True) / live_count
        inverse = 1.0 / jnp.sqrt(
            jnp.sum(centred * centred * live_col, axis=0, keepdims=True) / live_count + EPS
        )
        normed = centred * inverse
        before = normed + offset[None]
        active = jnp.maximum(before, 0.0)
        value_now = jnp.sum(active * output[None], axis=1)
        slope = weight * (value_now - target)
        grad_head = jnp.dot(slope, active)
        grad_unit = jnp.where(before > 0, slope[:, None] * output[None], 0.0)
        grad_shift = jnp.sum(grad_unit, axis=0)
        unit_mean = jnp.sum(grad_unit * live_col, axis=0, keepdims=True) / live_count
        cross_mean = jnp.sum(grad_unit * normed * live_col, axis=0, keepdims=True) / live_count
        grad_pre = (inverse * (grad_unit - unit_mean - normed * cross_mean) * live_col).astype(
            jnp.bfloat16
        )
        grad_w1 = jnp.dot(grad_pre.T, rows_in, preferred_element_type=jnp.float32)
        return (grad_w1, grad_shift, grad_head)

    grad_w1, grad_shift, grad_head = lax.map(critic, (critic_w1, critic_shift, critic_head))
    hidden = critic_w1.shape[1]
    root = jnp.float32(math.sqrt(total_critics * hidden * (width + 2)))
    grad_w1, grad_shift, grad_head = in_one((grad_w1, grad_shift, grad_head), "dp")
    squares = (
        jnp.sum(grad_w1 * grad_w1)
        + jnp.sum(grad_shift * grad_shift)
        + jnp.sum(grad_head * grad_head)
    )
    norm = jnp.sqrt(over_copies(squares, "member"))
    factor = root / jnp.maximum(norm, root)
    return (grad_w1 * factor, grad_shift * factor, grad_head * factor)


def solution(mesh):
    in_specs = (
        P("dp", None),
        P("dp", None),
        P("dp"),
        P("dp"),
        P("dp"),
        P("dp"),
        P(),
        P("dp", None),
        P("dp"),
        P("member", None, None),
        P("member", None),
        P("member", None),
        P("member", None, None),
        P("member", None),
        P("member", None),
        P("member", None),
        P("member", None),
    )
    out_specs = (P("member", None, None), P("member", None), P("member", None))
    return jax.shard_map(
        per_device, mesh=mesh, in_specs=in_specs, out_specs=out_specs, check_vma=False
    )
```

profile of v0, /device:TPU:1, one launch (start us, length us, event | category | flops | bytes accessed | tf_op | source)
XLA Modules:
  0.0 376.6 jit_solution(3712643342671129567)
XLA Ops:
  7.2 0.0 copy-start
  7.2 0.9 fusion.45
  8.0 0.8 copy-done
  8.8 0.0 copy-start.9
  8.8 4.7 %multiply_reduce_fusion.4 = f32[2,512]{1,0:T(2,128)S(1)} fusion(bf16[2,2048,256]{2,1,0:T(8,128)(2,1)S(1)} %copy-done, f32[2,2048]{1,0:T(2,128)} %param.35, f32[2,2048]{1,0:T(2,128)} %param.34, f32[2,2048]{1,0:T(2,128)} %param.33, f32[2,2048]{1,0:T(2,128)} %param.32, bf16[512,256]{1,0:T(8,128)(2,1)} %param.20), kind=kOutput, calls=%fused_computation.42 | convolution fusion | flops 1086323712 | bytes 2428928 | tf_op jit(solution)/shard_map/si,cfi->csf/dot_general | solution.py:76
  13.6 10.3 %all-gather = f32[4,2,512]{2,1,0:T(2,128)S(1)} all-gather(f32[1,2,512]{2,1,0:T(2,128)S(1)} %bitcast.140), channel_id=1, replica_groups=mesh['dp'=64,'member'=4] {'member'}, dimensions={0}, use_global_device_ids=true | all-gather | bytes 20480 | tf_op jit(solution)/shard_map/all_gather | solution.py:83
  23.9 1.2 reduce-window.6
  25.2 0.2 slice_reduce_fusion
  25.4 0.1 fusion.34
  25.6 3.8 %scatter_custom_fusion.2 = bf16[1024]{0:T(1024)(128)(2,1)S(1)} fusion(s32[512]{0:T(512)S(1)} %compare_select_fusion, bf16[512]{0:T(512)(128)(2,1)S(1)} %add_convert_fusion, bf16[]{:T(256)} %constant.21.clone.1), kind=kCustom, calls=%fused_computation.78 | custom fusion | bytes 2050 | tf_op jit(solution)/shard_map/scatter | solution.py:66
  29.4 0.7 all_to_all.26
  30.1 15.2 %all-to-all-start.2 = ((bf16[64,1,16]{2,1,0:T(2,128)(2,1)}), bf16[64,1,16]{2,1,0:T(2,128)(2,1)S(1)}, u32[]{:S(2)}, u32[]{:S(2)}) async-start(bf16[64,1,16]{2,1,0:T(2,128)(2,1)} %all_to_all.26), calls=%async_computation.2 | async-start | bytes 65536 | tf_op jit(solution)/shard_map/all_to_all | solution.py:95
  45.4 0.1 select_reduce_fusion
  45.4 3.8 scatter_custom_fusion.1
  49.2 0.7 all_to_all.25
  49.9 4.7 %all-to-all-done.2 = bf16[64,1,16]{2,1,0:T(2,128)(2,1)S(1)} async-done(((bf16[64,1,16]{2,1,0:T(2,128)(2,1)}), bf16[64,1,16]{2,1,0:T(2,128)(2,1)S(1)}, u32[]{:S(2)}, u32[]{:S(2)}) %all-to-all-start.2) | async-done | bytes 2080 | tf_op jit(solution)/shard_map/all_to_all | solution.py:95
  54.6 5.6 %all-to-all-start.1 = ((bf16[64,1,16]{2,1,0:T(2,128)(2,1)}), bf16[64,1,16]{2,1,0:T(2,128)(2,1)S(1)}, u32[]{:S(2)}, u32[]{:S(2)}) async-start(bf16[64,1,16]{2,1,0:T(2,128)(2,1)} %all_to_all.25), calls=%async_computation.1 | async-start | bytes 65536 | tf_op jit(solution)/shard_map/all_to_all | solution.py:94
  60.3 3.5 scatter_custom_fusion
  63.8 5.7 %all-to-all-done.1 = bf16[64,1,16]{2,1,0:T(2,128)(2,1)S(1)} async-done(((bf16[64,1,16]{2,1,0:T(2,128)(2,1)}), bf16[64,1,16]{2,1,0:T(2,128)(2,1)S(1)}, u32[]{:S(2)}, u32[]{:S(2)}) %all-to-all-start.1) | async-done | bytes 2080 | tf_op jit(solution)/shard_map/all_to_all | solution.py:94
  69.5 4.7 %all-to-all-start = ((bf16[64,16,256]{2,1,0:T(8,128)(2,1)}), bf16[64,16,256]{2,1,0:T(8,128)(2,1)S(1)}, u32[]{:S(2)}, u32[]{:S(2)}) async-start(bf16[64,16,256]{2,1,0:T(8,128)(2,1)} %bitcast.11), calls=%async_computation | async-start | bytes 1048576 | tf_op jit(solution)/shard_map/all_to_all | solution.py:93
  74.2 0.0 all-reduce.2.cloned.1.call-start
  74.3 3.8 %convert.6 = bf16[2,2048,256]{2,1,0:T(8,128)(2,1)} convert(f32[2,2048,256]{2,1,0:T(8,128)} %param.28) | non-fusion elementwise | flops 1048576 | bytes 6291456
  78.1 0.1 convert_reduce_fusion
  78.2 0.1 reshape.151
  78.3 0.8 convert_reduce_fusion.1
  79.1 0.1 reshape.152
  79.2 0.1 reshape.150
  79.2 12.3 %all-to-all-done = bf16[64,16,256]{2,1,0:T(8,128)(2,1)S(1)} async-done(((bf16[64,16,256]{2,1,0:T(8,128)(2,1)}), bf16[64,16,256]{2,1,0:T(8,128)(2,1)S(1)}, u32[]{:S(2)}, u32[]{:S(2)}) %all-to-all-start) | async-done | bytes 524320 | tf_op jit(solution)/shard_map/all_to_all | solution.py:93
  91.6 50.4 %while.14 = (s32[]{:T(128)}, f32[2,2048,256]{2,1,0:T(8,128)}, f32[2,2048]{1,0:T(2,128)S(1)}, f32[2,2048]{1,0:T(2,128)S(1)}, bf16[2,2048,256]{2,1,0:T(8,128)(2,1)...) while((s32[]{:T(128)}, f32[2,2048,256]{2,1,0:T(8,128)}, ...), condition=%wide.region_18.19_spmd, body=%wide.region_11.18_spmd.sunk | while | flops 2231370752 | bytes 92651704 | solution.py:129
  91.6 2.5 multiply_reduce_fusion.12
  94.2 0.7 broadcast_divide_fusion.5
  94.8 1.1 multiply_reduce_fusion.13
  96.0 0.7 add_rsqrt_fusion.2
  96.7 2.1 multiply_reduce_fusion.14
  98.7 1.4 fusion.63
  100.1 0.1 dynamic_update_slice.17
  100.2 7.7 %multiply_reduce_fusion.15 = (f32[2048]{0:T(1024)S(1)}, f32[2048]{0:T(1024)S(1)}, f32[2048]{0:T(1024)S(1)}, pred[1024,2048]{1,0:T(32,128)(4,1)}) fusion(f32[1024]{0:T(1024)S(1)} %bitcast.129, f32[1024]{0:T(1024)S(1)} %subtract_multiply_fusion.4, f32[2048]{0:T(1024)S(1)} %bitcast.125, f32[2048]{0:T(1024)S(1)} %add_rsqrt_fusion.2, ...), kind=kLoop, calls=%fused_computation.12.clone.1 | loop fusion | flops 25159680 | bytes 10551296 | tf_op jit(solution)/shard_map/while/body/eval_jaxpr/reduce_sum | solution.py:121
  107.9 0.1 dynamic_update_slice.16
  107.9 0.7 broadcast_divide_fusion.6
  108.6 8.2 %fusion.62 = f32[2,2048,256]{2,1,0:T(8,128)} fusion(f32[2,2048,256]{2,1,0:T(8,128)} %get-tuple-element.217, s32[]{:T(128)S(6)} %copy.44, bf16[1024,256]{1,0:T(8,128)(2,1)S(1)} %get-tuple-element.235, pred[1024,2048]{1,0:T(32,128)(4,1)} %get-tuple-element.196, f32[2048,1024]{0,1:T(8,128)} %copy-done.1, f32[2048]{0:T(1024)S(1)} %get-tuple-element.199, ...), kind=kOutput, calls=%fused_computation.28.clone.1 | convolution fusion | flops 1094713344 | bytes 13164548 | tf_op jit(solution)/shard_map/while/body/eval_jaxpr/dot_general | solution.py:126
  116.8 2.5 multiply_reduce_fusion.12
  119.4 0.7 broadcast_divide_fusion.5
  120.0 1.1 multiply_reduce_fusion.13
  121.2 0.7 add_rsqrt_fusion.2
  121.9 2.1 multiply_reduce_fusion.14
  124.0 1.4 fusion.63
  125.3 0.1 dynamic_update_slice.17
  125.4 7.7 %multiply_reduce_fusion.15 = (f32[2048]{0:T(1024)S(1)}, f32[2048]{0:T(1024)S(1)}, f32[2048]{0:T(1024)S(1)}, pred[1024,2048]{1,0:T(32,128)(4,1)}) fusion(f32[1024]{0:T(1024)S(1)} %bitcast.129, f32[1024]{0:T(1024)S(1)} %subtract_multiply_fusion.4, f32[2048]{0:T(1024)S(1)} %bitcast.125, f32[2048]{0:T(1024)S(1)} %add_rsqrt_fusion.2, ...), kind=kLoop, calls=%fused_computation.12.clone.1 | loop fusion | flops 25159680 | bytes 10551296 | tf_op jit(solution)/shard_map/while/body/eval_jaxpr/reduce_sum | solution.py:121
  133.1 0.1 dynamic_update_slice.16
  133.1 0.7 broadcast_divide_fusion.6
  133.8 8.2 %fusion.62 = f32[2,2048,256]{2,1,0:T(8,128)} fusion(f32[2,2048,256]{2,1,0:T(8,128)} %get-tuple-element.217, s32[]{:T(128)S(6)} %copy.44, bf16[1024,256]{1,0:T(8,128)(2,1)S(1)} %get-tuple-element.235, pred[1024,2048]{1,0:T(32,128)(4,1)} %get-tuple-element.196, f32[2048,1024]{0,1:T(8,128)} %copy-done.1, f32[2048]{0:T(1024)S(1)} %get-tuple-element.199, ...), kind=kOutput, calls=%fused_computation.28.clone.1 | convolution fusion | flops 1094713344 | bytes 13164548 | tf_op jit(solution)/shard_map/while/body/eval_jaxpr/dot_general | solution.py:126
  142.0 4.3 %copy.33 = f32[512,2,8,128]{3,1,2,0:T(2,128)S(1)} copy(f32[512,2,8,128]{3,2,1,0:T(8,128)} %bitcast.120) | data formatting | bytes 8388608
  146.3 4.4 %pad_maximum_fusion = f32[1056768]{0:T(1024)} fusion(f32[4096]{0:T(1024)S(1)} %bitcast.133, f32[4096]{0:T(1024)S(1)} %bitcast.134, f32[1048576]{0:T(1024)S(1)} %bitcast.119), kind=kLoop, calls=%fused_computation.43 | loop fusion | flops 2113536 | bytes 8454144 | tf_op jit(solution)/shard_map/concatenate | solution.py:17
  150.7 0.0 all-reduce.2.cloned.1.call-update
  150.7 191.0 %all-reduce.2.cloned.1.call-done = f32[1056768]{0:T(1024)} async-done(((f32[1056768]{0:T(1024)}), f32[1056768]{0:T(1024)}) %all-reduce.2.cloned.1.call-update) | async-done | bytes 4227088 | tf_op jit(solution)/shard_map/psum | solution.py:17
  341.8 3.9 %multiply_reduce_fusion.5 = f32[]{:T(128)} fusion(f32[1056768]{0:T(1024)} %all-reduce.2.cloned.1.call-done), kind=kLoop, calls=%fused_computation.44 | loop fusion | flops 2097151 | bytes 4194308 | tf_op jit(solution)/shard_map/reduce_sum | solution.py:134
  345.7 1.3 multiply_reduce_fusion.6
  349.0 7.9 %all_to_all.31 = f32[4,1,1]{2,1,0:T(1,128)S(1)} all-to-all(f32[4,1,1]{2,1,0:T(1,128)S(1)} %broadcast_in_dim.49), channel_id=1, replica_groups=mesh['dp'=64,'member'=4] {'member'}, dimensions={0} | all-to-all | bytes 32 | tf_op jit(solution)/shard_map/all_to_all | solution.py:23
  356.9 0.6 reduce_sum.153
  358.2 4.4 %slice_multiply_fusion = f32[1048576]{0:T(1024)} fusion(f32[1056768]{0:T(1024)} %all-reduce.2.cloned.1.call-done, f32[]{:T(128)S(6)} %div.42), kind=kLoop, calls=%fused_computation.45 | loop fusion | flops 1048576 | bytes 8388612 | tf_op jit(solution)/shard_map/mul | solution.py:140
  362.6 5.2 %mul.195 = f32[2,2048,256]{2,1,0:T(8,128)} reshape(f32[1048576]{0:T(1024)} %slice_multiply_fusion) | data formatting | bytes 8388608 | tf_op jit(solution)/shard_map/mul | solution.py:140
  367.8 0.7 slice_multiply_fusion.1
  368.5 0.6 mul.200
  369.2 0.6 mul.198
  (39 shorter events, 0.2 us)
Async XLA Ops:
  7.2 1.6 copy-start
  8.8 15.1 %copy-start.4 = (s32[512]{0:T(512)S(1)}, s32[512]{0:T(512)}, u32[]{:S(2)}) copy-start(s32[512]{0:T(512)} %param.27) | copy-start | bytes 6148
  8.8 16.8 %copy-start.6 = (s32[512]{0:T(512)S(1)}, s32[512]{0:T(512)}, u32[]{:S(2)}) copy-start(s32[512]{0:T(512)} %param.23) | copy-start | bytes 6148
  8.8 16.8 %copy-start.7 = (bf16[512]{0:T(512)(128)(2,1)S(1)}, bf16[512]{0:T(512)(128)(2,1)}, u32[]{:S(2)}) copy-start(bf16[512]{0:T(512)(128)(2,1)} %param.22) | copy-start | bytes 3076
  8.8 16.8 %copy-start.8 = (bf16[512]{0:T(512)(128)(2,1)S(1)}, bf16[512]{0:T(512)(128)(2,1)}, u32[]{:S(2)}) copy-start(bf16[512]{0:T(512)(128)(2,1)} %param.21) | copy-start | bytes 3076
  8.8 36.5 %copy-start.9 = (bf16[8]{0:T(256)(128)(2,1)S(1)}, bf16[8]{0:T(256)(128)(2,1)}, u32[]{:S(2)}) copy-start(bf16[8]{0:T(256)(128)(2,1)} %param.25) | copy-start | bytes 52
  8.8 36.5 %copy-start.5 = (s32[512]{0:T(512)S(1)}, s32[512]{0:T(512)}, u32[]{:S(2)}) copy-start(s32[512]{0:T(512)} %param.24) | copy-start | bytes 6148
  13.6 78.0 %copy-start.2 = (f32[2,2048]{1,0:T(2,128)S(1)}, f32[2,2048]{1,0:T(2,128)}, u32[]{:S(2)}) copy-start(f32[2,2048]{1,0:T(2,128)} %param.29) | copy-start | bytes 49156
  13.6 78.0 %copy-start.3 = (f32[2,2048]{1,0:T(2,128)S(1)}, f32[2,2048]{1,0:T(2,128)}, u32[]{:S(2)}) copy-start(f32[2,2048]{1,0:T(2,128)} %param.30) | copy-start | bytes 49156
  30.1 24.5 %all-to-all-start.2 = ((bf16[64,1,16]{2,1,0:T(2,128)(2,1)}), bf16[64,1,16]{2,1,0:T(2,128)(2,1)S(1)}, u32[]{:S(2)}, u32[]{:S(2)}) async-start(bf16[64,1,16]{2,1,0:T(2,128)(2,1)} %all_to_all.26), calls=%async_computation.2 | async-start | bytes 65536 | tf_op jit(solution)/shard_map/all_to_all | solution.py:95
  54.6 14.9 %all-to-all-start.1 = ((bf16[64,1,16]{2,1,0:T(2,128)(2,1)}), bf16[64,1,16]{2,1,0:T(2,128)(2,1)S(1)}, u32[]{:S(2)}, u32[]{:S(2)}) async-start(bf16[64,1,16]{2,1,0:T(2,128)(2,1)} %all_to_all.25), calls=%async_computation.1 | async-start | bytes 65536 | tf_op jit(solution)/shard_map/all_to_all | solution.py:94
  69.5 22.1 %all-to-all-start = ((bf16[64,16,256]{2,1,0:T(8,128)(2,1)}), bf16[64,16,256]{2,1,0:T(8,128)(2,1)S(1)}, u32[]{:S(2)}, u32[]{:S(2)}) async-start(bf16[64,16,256]{2,1,0:T(8,128)(2,1)} %bitcast.11), calls=%async_computation | async-start | bytes 1048576 | tf_op jit(solution)/shard_map/all_to_all | solution.py:93
  74.2 267.6 %all-reduce.2.cloned.1.call-start = ((), (), s32[]{:S(2)}) async-start(), calls=%async_computation.4 | async-start | bytes 8454144 | tf_op jit(solution)/shard_map/psum | solution.py:17
  94.1 4.6 %copy-start.1 = (f32[2048,1024]{0,1:T(8,128)}, f32[2048,1024]{0,1:T(8,128)S(1)}, u32[]{:S(2)}) copy-start(f32[2048,1024]{0,1:T(8,128)S(1)} %get-tuple-element.194) | copy-start | bytes 25165828 | tf_op jit(solution)/shard_map/while
  119.3 4.6 %copy-start.1 = (f32[2048,1024]{0,1:T(8,128)}, f32[2048,1024]{0,1:T(8,128)S(1)}, u32[]{:S(2)}) copy-start(f32[2048,1024]{0,1:T(8,128)S(1)} %get-tuple-element.194) | copy-start | bytes 25165828 | tf_op jit(solution)/shard_map/while
Sparse Core Ops, SparseCore 0:
  150.9 190.8 all-reduce.1
where the time goes:
time: 380 us; the launch traced here: 377 us
  waiting for transfers between devices  214 us (56%)
  other arithmetic  47.4 us (12%)
  matrix products  28.9 us (8%)
  local copies, waits for them, and re-layouts  25.7 us (7%)
  starting transfers between devices  25.6 us (7%)
  blocking collectives  18.2 us (5%)
  between operations  16.9 us (4%)
    psum x1, waiting for transfers between devices, in_one(): running = lax.psum(jnp.concatenate([a.ravel() for a in arrays]), axis)  191 us
    dot_general x2, matrix products, critic(): grad_w1 = jnp.dot(grad_pre.T, rows_in, preferred_element_type=jnp.float32)  16.4 us
    reduce_sum x2, other arithmetic, critic(): jnp.sum(grad_unit * live_col, axis=0, keepdims=True) / live_count  15.4 us
    all_to_all x1, starting transfers between devices, per_device(): lax.all_to_all(place(value), 'dp', split_axis=0, concat_axis=0, tiled=True)  15.2 us
    all_to_all x1, waiting for transfers between devices, per_device(): lax.all_to_all(place(features), 'dp', split_axis=0, concat_axis=0, tiled=...  12.3 us
    scatter x3, local copies, waits for them, and re-layouts, place(): empty.at[position].set(values)  11.1 us
    all_gather x1, blocking collectives, per_device(): everyone = lax.all_gather(mine, 'member', axis=1, tiled=True)  10.3 us
    all_to_all x1, blocking collectives, sent_to_all(): return lax.all_to_all(copies, axis, split_axis=0, concat_axis=0, tiled=True)  7.91 us
  transfers between devices with their start and end apart: 4, of which 4 were waited for; matrix products, arithmetic and copies ran while one was open for 3% of the time, Pallas kernels for 0%

commit v1 on v0

--- a/solution.py
+++ b/solution.py
@@ -1,31 +1,320 @@
+import functools
 import math
 
 import jax
 import jax.numpy as jnp
 from jax import lax
+from jax.experimental import pallas as pl
+from jax.experimental.pallas import tpu as pltpu
 from jax.sharding import PartitionSpec as P
 
 GAMMA = 0.99
 ALPHA = 0.2
 EPS = 1e-05
-
-
-def in_one(arrays, axis):
-    ends = [0]
-    for a in arrays:
-        ends.append(ends[-1] + a.size)
-    running = lax.psum(jnp.concatenate([a.ravel() for a in arrays]), axis)
-    return tuple((running[b:e].reshape(a.shape) for a, b, e in zip(arrays, ends, ends[1:])))
-
-
-def sent_to_all(array, axis):
-    copies = jnp.broadcast_to(array, (lax.axis_size(axis), *array.shape))
-    return lax.all_to_all(copies, axis, split_axis=0, concat_axis=0, tiled=True)
-
-
-def over_copies(array, axis):
-    everything = sent_to_all(array, axis)
-    return jnp.sum(everything, axis=0)
+NZ = 8
+MESH = pl.DeviceIdType.MESH
+
+
+def far_first(i, nz):
+    half = nz // 2
+    return half + ((i + 1) // 2) * (2 * ((i + 1) % 2) - 1)
+
+
+def near_first(i, nz):
+    return far_first(nz - 2 - i, nz)
+
+
+def reduce_kernel(
+    ny,
+    nz,
+    nx,
+    h,
+    hs,
+    full,
+    small,
+    total,
+    y_in,
+    z_out,
+    z_in,
+    ys_in,
+    zs_out,
+    zs_in,
+    x_out,
+    x_in,
+    y_sems,
+    z_sems,
+    gz_sems,
+    gy_sems,
+    pair_sems,
+    ys_sems,
+    zs_sems,
+    gzs_sems,
+    gys_sems,
+    pair_small,
+    x_sems,
+):
+    me = lax.axis_index("dp")
+    mx = lax.axis_index("member")
+    c = lax.rem(me, 2)
+    z = lax.rem(me // 2, nz)
+    y = me // (2 * nz)
+    partner = me + 1 - 2 * c
+
+    def dp_of(yy, zz):
+        return (yy * nz + zz) * 2 + c
+
+    def yo(o):
+        return lax.rem(y + o, ny)
+
+    def zo(o):
+        return lax.rem(z + o, nz)
+
+    def copy(src, dst, sems, index, dp):
+        return pltpu.make_async_remote_copy(
+            src_ref=src,
+            dst_ref=dst,
+            send_sem=sems.at[(0,) + index],
+            recv_sem=sems.at[(1,) + index],
+            device_id={"dp": dp},
+            device_id_type=MESH,
+        )
+
+    barrier = pltpu.get_barrier_semaphore()
+    for o in range(1, ny):
+        pl.semaphore_signal(barrier, inc=1, device_id={"dp": dp_of(yo(o), z)}, device_id_type=MESH)
+    for o in range(1, nz):
+        pl.semaphore_signal(barrier, inc=1, device_id={"dp": dp_of(y, zo(o))}, device_id_type=MESH)
+    pl.semaphore_signal(barrier, inc=1, device_id={"dp": partner}, device_id_type=MESH)
+    for o in range(1, nx):
+        pl.semaphore_signal(
+            barrier, inc=1, device_id={"member": lax.rem(mx + o, nx)}, device_id_type=MESH
+        )
+    pl.semaphore_wait(barrier, ny + nz + nx - 2)
+
+    def y_small(o):
+        return copy(hs.at[yo(o)], ys_in.at[o - 1], ys_sems, (o - 1,), dp_of(yo(o), z))
+
+    def y_block(o, oz):
+        return copy(
+            h.at[yo(o), zo(oz)],
+            y_in.at[o - 1, oz],
+            y_sems,
+            (o - 1, oz),
+            dp_of(yo(o), z),
+        )
+
+    for o in range(1, ny):
+        y_small(o).start()
+
+    def send_y(i, _):
+        oz = lax.rem(far_first(i, nz), nz)
+        for o in range(1, ny):
+            y_block(o, oz).start()
+        return 0
+
+    lax.fori_loop(0, nz - 1, send_y, 0)
+    for o in range(1, ny):
+        y_block(o, 0).start()
+
+    def z_small(o):
+        return copy(zs_out.at[zo(o)], zs_in.at[o - 1], zs_sems, (o - 1,), dp_of(y, zo(o)))
+
+    def z_block(o):
+        return copy(z_out.at[o], z_in.at[o], z_sems, (o,), dp_of(y, zo(o)))
+
+    for o in range(1, ny):
+        y_small(o).wait_recv()
+    zs_out[...] = hs[y] + sum(ys_in[o - 1] for o in range(1, ny))
+    for o in range(1, nz):
+        z_small(o).start()
+
+    def y_sum(oz):
+        for o in range(1, ny):
+            y_block(o, oz).wait_recv()
+        value = h[y, zo(oz)].astype(jnp.float32)
+        for o in range(1, ny):
+            value = value + y_in[o - 1, oz].astype(jnp.float32)
+        z_out[oz] = value
+
+    def send_z(i, _):
+        oz = lax.rem(far_first(i, nz), nz)
+        y_sum(oz)
+        z_block(oz).start()
+        return 0
+
+    lax.fori_loop(0, nz - 1, send_z, 0)
+    y_sum(0)
+
+    for o in range(1, nz):
+        z_small(o).wait_recv()
+    mine_small = zs_out[z] + sum(zs_in[o - 1] for o in range(1, nz))
+
+    def add_z(i, value):
+        oz = near_first(i, nz)
+        z_block(oz).wait_recv()
+        return value + z_in[oz]
+
+    z_out[0] = lax.fori_loop(0, nz - 1, add_z, z_out[0])
+    mine = z_out[0]
+    squares = jnp.sum(mine * mine) + jnp.sum(mine_small * mine_small)
+    small[c, y, z, :, 0:128] = mine_small
+    small[c, y, z, :, 128:256] = jnp.full((1, 128), squares, jnp.float32)
+    full[c, y, z] = mine.astype(jnp.bfloat16)
+
+    def gz_small(o):
+        ref = small.at[c, y, z]
+        return copy(ref, ref, gzs_sems, (o - 1,), dp_of(y, zo(o)))
+
+    def gz_block(o):
+        ref = full.at[c, y, z]
+        return copy(ref, ref, gz_sems, (o,), dp_of(y, zo(o)))
+
+    def gy_small(o):
+        ref = small.at[c, y]
+        return copy(ref, ref, gys_sems, (o - 1,), dp_of(yo(o), z))
+
+    def gy_block(o, oz):
+        ref = full.at[c, y, zo(nz - oz)]
+        return copy(ref, ref, gy_sems, (o - 1, oz), dp_of(yo(o), z))
+
+    def pair_block(oy, oz):
+        ref = full.at[c, yo(ny - oy), zo(nz - oz)]
+        return copy(ref, ref, pair_sems, (oy, oz), partner)
+
+    for o in range(1, nz):
+        gz_small(o).start()
+
+    def send_gz(i, _):
+        gz_block(far_first(i, nz)).start()
+        return 0
+
+    lax.fori_loop(0, nz - 1, send_gz, 0)
+    for o in range(1, ny):
+        gy_block(o, 0).start()
+    pair_block(0, 0).start()
+
+    for o in range(1, nz):
+        gz_small(o).wait_recv()
+    for o in range(1, ny):
+        gy_small(o).start()
+
+    def relay_z(i, _):
+        oz = near_first(i, nz)
+        gz_block(oz).wait_recv()
+        for o in range(1, ny):
+            gy_block(o, oz).start()
+        pair_block(0, oz).start()
+        return 0
+
+    lax.fori_loop(0, nz - 1, relay_z, 0)
+
+    for o in range(1, ny):
+        gy_small(o).wait_recv()
+    pair_s = copy(small.at[c], small.at[c], pair_small, (0,), partner)
+    pair_s.start()
+
+    def relay_y(i, _):
+        oz = lax.rem(near_first(lax.rem(i + nz - 2, nz - 1), nz) * lax.min(i, 1), nz)
+        for o in range(1, ny):
+            gy_block(o, oz).wait_recv()
+            pair_block(o, oz).start()
+        return 0
+
+    half = nz // 2
+    lax.fori_loop(0, half, relay_y, 0)
+    pair_s.wait_recv()
+    x_out[...] = jnp.sum(small[:, :, :, :, 128:256], axis=(0, 1, 2))
+
+    def x_copy(o):
+        return pltpu.make_async_remote_copy(
+            src_ref=x_out,
+            dst_ref=x_in.at[o - 1],
+            send_sem=x_sems.at[0, o - 1],
+            recv_sem=x_sems.at[1, o - 1],
+            device_id={"member": lax.rem(mx + o, nx)},
+            device_id_type=MESH,
+        )
+
+    for o in range(1, nx):
+        x_copy(o).start()
+    lax.fori_loop(half, nz, relay_y, 0)
+    for o in range(1, nx):
+        x_copy(o).wait_recv()
+    total[...] = x_out[...] + sum(x_in[o - 1] for o in range(1, nx))
+
+    def wait_pair(i, _):
+        for o in range(ny):
+            pair_block(o, i).wait_recv()
+        return 0
+
+    lax.fori_loop(0, nz, wait_pair, 0)
+
+    def drain_y(i, _):
+        for o in range(1, ny):
+            y_block(o, i).wait_send()
+            gy_block(o, i).wait_send()
+        for o in range(ny):
+            pair_block(o, i).wait_send()
+        return 0
+
+    lax.fori_loop(0, nz, drain_y, 0)
+
+    def drain_z(i, _):
+        z_block(i).wait_send()
+        gz_block(i).wait_send()
+        return 0
+
+    lax.fori_loop(1, nz, drain_z, 0)
+    for o in range(1, ny):
+        y_small(o).wait_send()
+        gy_small(o).wait_send()
+    for o in range(1, nz):
+        z_small(o).wait_send()
+        gz_small(o).wait_send()
+    for o in range(1, nx):
+        x_copy(o).wait_send()
+    pair_s.wait_send()
+
+
+def reduce_all(h, hs, ny, nz, nx):
+    rows, width = h.shape[2:]
+    f32, bf16 = jnp.float32, jnp.bfloat16
+    vmem = pl.BlockSpec(memory_space=pltpu.VMEM)
+    dma = pltpu.SemaphoreType.DMA
+    return pl.pallas_call(
+        functools.partial(reduce_kernel, ny, nz, nx),
+        out_shape=(
+            jax.ShapeDtypeStruct((2, ny, nz, rows, width), bf16),
+            jax.ShapeDtypeStruct((2, ny, nz, 1, 256), f32),
+            jax.ShapeDtypeStruct((1, 128), f32),
+        ),
+        in_specs=[vmem] * 2,
+        out_specs=[vmem] * 3,
+        scratch_shapes=[
+            pltpu.VMEM((ny - 1, nz, rows, width), bf16),
+            pltpu.VMEM((nz, rows, width), f32),
+            pltpu.VMEM((nz, rows, width), f32),
+            pltpu.VMEM((ny - 1, nz, 1, 128), f32),
+            pltpu.VMEM((nz, 1, 128), f32),
+            pltpu.VMEM((nz - 1, 1, 128), f32),
+            pltpu.VMEM((1, 128), f32),
+            pltpu.VMEM((nx - 1, 1, 128), f32),
+            dma((2, ny - 1, nz)),
+            dma((2, nz)),
+            dma((2, nz)),
+            dma((2, ny - 1, nz)),
+            dma((2, ny, nz)),
+            dma((2, ny - 1)),
+            dma((2, nz - 1)),
+            dma((2, nz - 1)),
+            dma((2, ny - 1)),
+            dma((2, 1)),
+            dma((2, nx - 1)),
+        ],
+        compiler_params=pltpu.CompilerParams(collective_id=0, has_side_effects=True),
+        cost_estimate=pl.CostEstimate(flops=10**7, bytes_accessed=4 * 10**6, transcendentals=0),
+        name="gradient_sum",
+    )(h, hs)
 
 
 def per_device(
@@ -129,15 +418,34 @@
     grad_w1, grad_shift, grad_head = lax.map(critic, (critic_w1, critic_shift, critic_head))
     hidden = critic_w1.shape[1]
     root = jnp.float32(math.sqrt(total_critics * hidden * (width + 2)))
-    grad_w1, grad_shift, grad_head = in_one((grad_w1, grad_shift, grad_head), "dp")
-    squares = (
-        jnp.sum(grad_w1 * grad_w1)
-        + jnp.sum(grad_shift * grad_shift)
-        + jnp.sum(grad_head * grad_head)
-    )
-    norm = jnp.sqrt(over_copies(squares, "member"))
+    nz = NZ
+    ny = shards // (2 * nz)
+    blocks = ny * nz
+    core = lax.rem(lax.axis_index("dp"), 2)
+    pairs = [(i, i ^ 1) for i in range(shards)]
+
+    def half_sum(a):
+        keep = lax.dynamic_index_in_dim(a, core, 0, keepdims=False)
+        give = lax.dynamic_index_in_dim(a, 1 - core, 0, keepdims=False)
+        return keep + lax.ppermute(give, "dp", pairs)
+
+    h = half_sum(grad_w1).astype(jnp.bfloat16).reshape(ny, nz, hidden // blocks, width)
+    vectors = jnp.concatenate(
+        [
+            grad_shift.reshape(2, blocks, hidden // blocks),
+            grad_head.reshape(2, blocks, hidden // blocks),
+        ],
+        axis=2,
+    )
+    hs = half_sum(vectors).reshape(ny, nz, 1, 2 * hidden // blocks)
+    full, small, squares = reduce_all(h, hs, ny, nz, members)
+    norm = jnp.sqrt(squares[0, 0])
     factor = root / jnp.maximum(norm, root)
-    return (grad_w1 * factor, grad_shift * factor, grad_head * factor)
+    step_w1 = full.reshape(2, hidden, width).astype(jnp.float32) * factor
+    per = hidden // blocks
+    step_shift = small[..., 0, 0:per].reshape(2, hidden) * factor
+    step_head = small[..., 0, per : 2 * per].reshape(2, hidden) * factor
+    return (step_w1, step_shift, step_head)
 
 
 def solution(mesh):

time: 380 us -> 203 us (0.53)
  waiting for transfers between devices: 214 us -> 26.3 us
  Pallas kernels: 0 us -> 47.3 us
  between operations: 16.9 us -> 1.5 us
  blocking collectives: 18.2 us -> 10.3 us
  local copies, waits for them, and re-layouts: 25.7 us -> 19.5 us
  other arithmetic: 47.4 us -> 41.4 us
    psum x1 -> x0, waiting for transfers between devices: 191 us -> none  [in_one(): running = lax.psum(jnp.concatenate([a.ravel() for a in arrays]), axis)]
    pallas_call x0 -> x1, Pallas kernels: none -> 47.3 us  [reduce_all(): pl.pallas_call(functools.partial(reduce_kernel, ny, nz, nx), out_shape=(j...]
    all_to_all x1 -> x0, blocking collectives: 7.91 us -> none  [sent_to_all(): return lax.all_to_all(copies, axis, split_axis=0, concat_axis=0, tiled=True)]
    reduce_sum x3 -> x0, other arithmetic: 5.82 us -> none  [the longest x1 3.87 us: per_device(): jnp.sum(grad_w1 * grad_w1) + jnp.sum(grad_shift * grad_shift)]
    mul x3 -> x2, local copies, waits for them, and re-layouts: 6.41 us -> 1.38 us  [the longest x1 0.69 us: per_device(): step_head = small[..., 0, per:2 * per].reshape(2, hidden) * factor]
    concatenate x1 -> x0, other arithmetic: 4.38 us -> none  [in_one(): running = lax.psum(jnp.concatenate([a.ravel() for a in arrays]), axis)]
    unnamed x22 -> x19, local copies, waits for them, and re-layouts: 5.17 us -> 0.82 us
  transfers between devices with their start and end apart: 4 -> 5, of which waited for: 4 -> 4; matrix products, arithmetic and copies ran while one was open for 3% -> 7% of each run, Pallas kernels for 0% -> 0%
where the time goes in v1:
time: 203 us; the launch traced here: 202 us
  Pallas kernels  47.3 us (23%)
  other arithmetic  41.4 us (20%)
  matrix products  28.9 us (14%)
  starting transfers between devices  26.3 us (13%)
  waiting for transfers between devices  26.3 us (13%)
  local copies, waits for them, and re-layouts  19.5 us (10%)
  blocking collectives  10.3 us (5%)
    pallas_call x1, Pallas kernels, reduce_all(): pl.pallas_call(functools.partial(reduce_kernel, ny, nz, nx), out_shape=(j...  47.3 us
    dot_general x2, matrix products, critic(): grad_w1 = jnp.dot(grad_pre.T, rows_in, preferred_element_type=jnp.float32)  16.4 us
    reduce_sum x2, other arithmetic, critic(): jnp.sum(grad_unit * live_col, axis=0, keepdims=True) / live_count  15.4 us
    all_to_all x1, starting transfers between devices, per_device(): lax.all_to_all(place(value), 'dp', split_axis=0, concat_axis=0, tiled=True)  15.2 us
    all_to_all x1, waiting for transfers between devices, per_device(): lax.all_to_all(place(features), 'dp', split_axis=0, concat_axis=0, tiled=...  12.4 us
    scatter x3, local copies, waits for them, and re-layouts, place(): empty.at[position].set(values)  11.1 us
    all_gather x1, blocking collectives, per_device(): everyone = lax.all_gather(mine, 'member', axis=1, tiled=True)  10.3 us
    all_to_all x1, waiting for transfers between devices, per_device(): lax.all_to_all(place(weight_rows), 'dp', split_axis=0, concat_axis=0, til...  5.71 us
  transfers between devices with their start and end apart: 5, of which 4 were waited for; matrix products, arithmetic and copies ran while one was open for 7% of the time, Pallas kernels for 0%

profile of v1, /device:TPU:1, one launch (start us, length us, event | category | flops | bytes accessed | tf_op | source)
XLA Modules:
  0.0 201.7 jit_solution(6086538860822390868)
XLA Ops:
  0.6 0.0 copy-start
  0.6 0.9 fusion.51
  1.5 0.8 copy-done
  2.3 4.7 %multiply_reduce_fusion.4 = f32[2,512]{1,0:T(2,128)S(1)} fusion(bf16[2,2048,256]{2,1,0:T(8,128)(2,1)S(1)} %copy-done, f32[2,2048]{1,0:T(2,128)} %param.35, f32[2,2048]{1,0:T(2,128)} %param.34, f32[2,2048]{1,0:T(2,128)} %param.33, f32[2,2048]{1,0:T(2,128)} %param.32, bf16[512,256]{1,0:T(8,128)(2,1)} %param.20), kind=kOutput, calls=%fused_computation.42 | convolution fusion | flops 1086323712 | bytes 2428928 | tf_op jit(solution)/shard_map/si,cfi->csf/dot_general | solution.py:365
  7.0 0.0 copy-start.2
  7.1 10.3 %all-gather = f32[4,2,512]{2,1,0:T(2,128)S(1)} all-gather(f32[1,2,512]{2,1,0:T(2,128)S(1)} %bitcast.152), channel_id=1, replica_groups=mesh['dp'=64,'member'=4] {'member'}, dimensions={0}, use_global_device_ids=true | all-gather | bytes 20480 | tf_op jit(solution)/shard_map/all_gather | solution.py:372
  17.4 1.2 reduce-window.6
  18.6 0.2 slice_reduce_fusion
  18.9 0.1 fusion.35
  19.1 3.8 %scatter_custom_fusion.2 = bf16[1024]{0:T(1024)(128)(2,1)S(1)} fusion(s32[512]{0:T(512)S(1)} %compare_select_fusion, bf16[512]{0:T(512)(128)(2,1)S(1)} %add_convert_fusion, bf16[]{:T(256)} %constant.42.clone.1), kind=kCustom, calls=%fused_computation.86 | custom fusion | bytes 2050 | tf_op jit(solution)/shard_map/scatter | solution.py:355
  22.9 0.7 all_to_all.21
  23.6 15.2 %all-to-all-start.2 = ((bf16[64,1,16]{2,1,0:T(2,128)(2,1)}), bf16[64,1,16]{2,1,0:T(2,128)(2,1)S(1)}, u32[]{:S(2)}, u32[]{:S(2)}) async-start(bf16[64,1,16]{2,1,0:T(2,128)(2,1)} %all_to_all.21), calls=%async_computation.2 | async-start | bytes 65536 | tf_op jit(solution)/shard_map/all_to_all | solution.py:384
  38.8 0.1 select_reduce_fusion
  38.9 3.8 %scatter_custom_fusion.1 = bf16[1024]{0:T(1024)(128)(2,1)S(1)} fusion(s32[512]{0:T(512)S(1)} %compare_select_fusion, bf16[512]{0:T(512)(128)(2,1)S(1)} %select_reduce_fusion, bf16[]{:T(256)} %constant.42.clone.1), kind=kCustom, calls=%fused_computation.88 | custom fusion | bytes 2050 | tf_op jit(solution)/shard_map/scatter | solution.py:355
  42.7 0.7 all_to_all.20
  43.4 4.7 %all-to-all-done.2 = bf16[64,1,16]{2,1,0:T(2,128)(2,1)S(1)} async-done(((bf16[64,1,16]{2,1,0:T(2,128)(2,1)}), bf16[64,1,16]{2,1,0:T(2,128)(2,1)S(1)}, u32[]{:S(2)}, u32[]{:S(2)}) %all-to-all-start.2) | async-done | bytes 2080 | tf_op jit(solution)/shard_map/all_to_all | solution.py:384
  48.1 5.6 %all-to-all-start.1 = ((bf16[64,1,16]{2,1,0:T(2,128)(2,1)}), bf16[64,1,16]{2,1,0:T(2,128)(2,1)S(1)}, u32[]{:S(2)}, u32[]{:S(2)}) async-start(bf16[64,1,16]{2,1,0:T(2,128)(2,1)} %all_to_all.20), calls=%async_computation.1 | async-start | bytes 65536 | tf_op jit(solution)/shard_map/all_to_all | solution.py:383
  53.7 3.5 %scatter_custom_fusion = bf16[1024,256]{1,0:T(8,128)(2,1)} fusion(s32[512]{0:T(512)S(1)} %compare_select_fusion, bf16[512,256]{1,0:T(8,128)(2,1)} %param.19, bf16[]{:T(256)} %constant.42.clone.1), kind=kCustom, calls=%fused_computation.48 | custom fusion | bytes 524800 | tf_op jit(solution)/shard_map/scatter | solution.py:355
  57.2 5.7 %all-to-all-done.1 = bf16[64,1,16]{2,1,0:T(2,128)(2,1)S(1)} async-done(((bf16[64,1,16]{2,1,0:T(2,128)(2,1)}), bf16[64,1,16]{2,1,0:T(2,128)(2,1)S(1)}, u32[]{:S(2)}, u32[]{:S(2)}) %all-to-all-start.1) | async-done | bytes 2080 | tf_op jit(solution)/shard_map/all_to_all | solution.py:383
  63.0 4.7 %all-to-all-start = ((bf16[64,16,256]{2,1,0:T(8,128)(2,1)}), bf16[64,16,256]{2,1,0:T(8,128)(2,1)S(1)}, u32[]{:S(2)}, u32[]{:S(2)}) async-start(bf16[64,16,256]{2,1,0:T(8,128)(2,1)} %bitcast.11), calls=%async_computation | async-start | bytes 1048576 | tf_op jit(solution)/shard_map/all_to_all | solution.py:382
  67.7 3.8 %convert.6 = bf16[2,2048,256]{2,1,0:T(8,128)(2,1)} convert(f32[2,2048,256]{2,1,0:T(8,128)} %param.28) | non-fusion elementwise | flops 1048576 | bytes 6291456
  71.5 0.1 convert_reduce_fusion
  71.6 0.1 reshape.139
  71.7 0.8 convert_reduce_fusion.1
  72.5 0.1 reshape.140
  72.6 0.1 reshape.138
  72.7 12.4 %all-to-all-done = bf16[64,16,256]{2,1,0:T(8,128)(2,1)S(1)} async-done(((bf16[64,16,256]{2,1,0:T(8,128)(2,1)}), bf16[64,16,256]{2,1,0:T(8,128)(2,1)S(1)}, u32[]{:S(2)}, u32[]{:S(2)}) %all-to-all-start) | async-done | bytes 524320 | tf_op jit(solution)/shard_map/all_to_all | solution.py:382
  85.0 50.4 %while.14 = (s32[]{:T(128)}, f32[2,2048,256]{2,1,0:T(8,128)}, f32[2,2048]{1,0:T(2,128)S(1)}, f32[2,2048]{1,0:T(2,128)S(1)}, bf16[2,2048,256]{2,1,0:T(8,128)(2,1)...) while((s32[]{:T(128)}, f32[2,2048,256]{2,1,0:T(8,128)}, ...), condition=%wide.region_18.19_spmd, body=%wide.region_11.18_spmd.sunk | while | flops 2231370752 | bytes 92651704 | solution.py:418
  85.1 2.5 %multiply_reduce_fusion.11 = (f32[2048]{0:T(1024)S(1)}, f32[2048,1024]{0,1:T(8,128)S(1)}) fusion(f32[1024]{0:T(1024)S(1)} %bitcast.142, bf16[1024,256]{1,0:T(8,128)(2,1)S(1)} %get-tuple-element.239, bf16[2,2048,256]{2,1,0:T(8,128)(2,1)} %get-tuple-element.238, s32[]{:T(128)S(6)} %copy.33), kind=kOutput, calls=%fused_computation.17.clone.1 | convolution fusion | flops 1077934080 | bytes 9973764 | tf_op jit(solution)/shard_map/while/body/eval_jaxpr/dot_general | solution.py:395
  87.6 0.7 broadcast_divide_fusion.5
  88.3 1.1 multiply_reduce_fusion.12
  89.4 0.7 add_rsqrt_fusion.2
  90.1 2.1 %multiply_reduce_fusion.13 = f32[1024]{0:T(1024)S(1)} fusion(f32[2048,1024]{0,1:T(8,128)S(1)} %get-tuple-element.198, f32[2048]{0:T(1024)S(1)} %bitcast.139, f32[2048]{0:T(1024)S(1)} %bitcast.136, f32[2048]{0:T(1024)S(1)} %add_rsqrt_fusion.2, f32[2048]{0:T(1024)S(1)} %broadcast_divide_fusion.5), kind=kLoop, calls=%fused_computation.15.clone.1 | loop fusion | flops 12581888 | bytes 8425472 | tf_op jit(solution)/shard_map/while/body/eval_jaxpr/reduce_sum | solution.py:405
  92.2 1.4 fusion.69
  93.6 0.1 dynamic_update_slice.17
  93.6 7.7 %multiply_reduce_fusion.14 = (f32[2048]{0:T(1024)S(1)}, f32[2048]{0:T(1024)S(1)}, f32[2048]{0:T(1024)S(1)}, pred[1024,2048]{1,0:T(32,128)(4,1)}) fusion(f32[1024]{0:T(1024)S(1)} %bitcast.144, f32[1024]{0:T(1024)S(1)} %subtract_multiply_fusion.4, f32[2048]{0:T(1024)S(1)} %bitcast.140, f32[2048]{0:T(1024)S(1)} %add_rsqrt_fusion.2, ...), kind=kLoop, calls=%fused_computation.12.clone.1 | loop fusion | flops 25159680 | bytes 10551296 | tf_op jit(solution)/shard_map/while/body/eval_jaxpr/reduce_sum | solution.py:410
  101.3 0.1 dynamic_update_slice.16
  101.4 0.7 broadcast_divide_fusion.6
  102.0 8.2 %fusion.68 = f32[2,2048,256]{2,1,0:T(8,128)} fusion(f32[2,2048,256]{2,1,0:T(8,128)} %get-tuple-element.221, s32[]{:T(128)S(6)} %copy.33, bf16[1024,256]{1,0:T(8,128)(2,1)S(1)} %get-tuple-element.239, pred[1024,2048]{1,0:T(32,128)(4,1)} %get-tuple-element.200, f32[2048,1024]{0,1:T(8,128)} %copy-done.1, f32[2048]{0:T(1024)S(1)} %get-tuple-element.203, ...), kind=kOutput, calls=%fused_computation.28.clone.1 | convolution fusion | flops 1094713344 | bytes 13164548 | tf_op jit(solution)/shard_map/while/body/eval_jaxpr/dot_general | solution.py:415
  110.3 2.5 %multiply_reduce_fusion.11 = (f32[2048]{0:T(1024)S(1)}, f32[2048,1024]{0,1:T(8,128)S(1)}) fusion(f32[1024]{0:T(1024)S(1)} %bitcast.142, bf16[1024,256]{1,0:T(8,128)(2,1)S(1)} %get-tuple-element.239, bf16[2,2048,256]{2,1,0:T(8,128)(2,1)} %get-tuple-element.238, s32[]{:T(128)S(6)} %copy.33), kind=kOutput, calls=%fused_computation.17.clone.1 | convolution fusion | flops 1077934080 | bytes 9973764 | tf_op jit(solution)/shard_map/while/body/eval_jaxpr/dot_general | solution.py:395
  112.8 0.7 broadcast_divide_fusion.5
  113.5 1.1 multiply_reduce_fusion.12
  114.6 0.7 add_rsqrt_fusion.2
  115.3 2.1 %multiply_reduce_fusion.13 = f32[1024]{0:T(1024)S(1)} fusion(f32[2048,1024]{0,1:T(8,128)S(1)} %get-tuple-element.198, f32[2048]{0:T(1024)S(1)} %bitcast.139, f32[2048]{0:T(1024)S(1)} %bitcast.136, f32[2048]{0:T(1024)S(1)} %add_rsqrt_fusion.2, f32[2048]{0:T(1024)S(1)} %broadcast_divide_fusion.5), kind=kLoop, calls=%fused_computation.15.clone.1 | loop fusion | flops 12581888 | bytes 8425472 | tf_op jit(solution)/shard_map/while/body/eval_jaxpr/reduce_sum | solution.py:405
  117.4 1.4 fusion.69
  118.8 0.1 dynamic_update_slice.17
  118.8 7.7 %multiply_reduce_fusion.14 = (f32[2048]{0:T(1024)S(1)}, f32[2048]{0:T(1024)S(1)}, f32[2048]{0:T(1024)S(1)}, pred[1024,2048]{1,0:T(32,128)(4,1)}) fusion(f32[1024]{0:T(1024)S(1)} %bitcast.144, f32[1024]{0:T(1024)S(1)} %subtract_multiply_fusion.4, f32[2048]{0:T(1024)S(1)} %bitcast.140, f32[2048]{0:T(1024)S(1)} %add_rsqrt_fusion.2, ...), kind=kLoop, calls=%fused_computation.12.clone.1 | loop fusion | flops 25159680 | bytes 10551296 | tf_op jit(solution)/shard_map/while/body/eval_jaxpr/reduce_sum | solution.py:410
  126.5 0.1 dynamic_update_slice.16
  126.6 0.7 broadcast_divide_fusion.6
  127.3 8.2 %fusion.68 = f32[2,2048,256]{2,1,0:T(8,128)} fusion(f32[2,2048,256]{2,1,0:T(8,128)} %get-tuple-element.221, s32[]{:T(128)S(6)} %copy.33, bf16[1024,256]{1,0:T(8,128)(2,1)S(1)} %get-tuple-element.239, pred[1024,2048]{1,0:T(32,128)(4,1)} %get-tuple-element.200, f32[2048,1024]{0,1:T(8,128)} %copy-done.1, f32[2048]{0:T(1024)S(1)} %get-tuple-element.203, ...), kind=kOutput, calls=%fused_computation.28.clone.1 | convolution fusion | flops 1094713344 | bytes 13164548 | tf_op jit(solution)/shard_map/while/body/eval_jaxpr/dot_general | solution.py:415
  135.4 3.0 %dynamic-slice_bitcast_fusion = f32[2048,256]{1,0:T(8,128)} fusion(f32[2,2048,256]{2,1,0:T(8,128)} %get-tuple-element.70, s32[]{:T(128)S(6)} %select_n.35), kind=kLoop, calls=%fused_computation.46 | loop fusion | bytes 4194308 | tf_op jit(solution)/shard_map/jit(dynamic_index_in_dim)/squeeze | solution.py:429
  138.5 0.3 collective-permute-start
  138.7 0.1 reshape.136
  138.8 0.1 reshape.135
  138.9 0.1 fusion.40
  139.0 0.5 collective-permute-start.1
  139.5 3.5 %collective-permute-done.1 = f32[32,128]{1,0:T(8,128)S(1)} collective-permute-done((f32[32,128]{1,0:T(8,128)S(1)}, f32[32,128]{1,0:T(8,128)S(1)}, u32[]{:S(2)}, u32[]{:S(2)}) %collective-permute-start.1) | collective-permute-done | bytes 16416 | tf_op jit(solution)/shard_map/ppermute | solution.py:430
  143.0 0.7 fusion.43
  143.7 3.4 %fusion.29 = bf16[2048,256]{1,0:T(8,128)(2,1)} fusion(f32[2048,256]{1,0:T(8,128)} %collective-permute-done, f32[2,2048,256]{2,1,0:T(8,128)} %get-tuple-element.70, s32[]{:T(128)S(6)} %select_n.34), kind=kLoop, calls=%fused_computation.45 | loop fusion | flops 1048576 | bytes 5242884 | tf_op jit(solution)/shard_map/convert_element_type | solution.py:432
  147.1 47.3 %gradient_sum.1 = (bf16[2,4,8,64,256]{4,3,2,1,0:T(8,128)(2,1)}, f32[2,4,8,1,256]{4,3,2,1,0:T(1,128)}, f32[1,128]{1,0:T(1,128)}) custom-call(bf16[4,8,64,256]{3,2,1,0:T(8,128)(2,1)} %bitcast.135, f32[4,8,1,128]{3,2,1,0:T(1,128)} %bitcast.148), custom_call_target="tpu_custom_call" | custom-call | flops 10000000 | bytes 4000000 | tf_op jit(solution)/shard_map/gradient_sum/pallas_call | solution.py:284
  195.0 1.1 multiply_reduce_fusion.5
  196.1 0.7 mul.185
  196.8 0.7 mul.183
  197.5 4.2 %convert_multiply_fusion = f32[2,4,8,64,256]{4,3,2,1,0:T(8,128)} fusion(bf16[2,4,8,64,256]{4,3,2,1,0:T(8,128)(2,1)} %get-tuple-element.73, f32[]{:T(128)} %bitcast.24), kind=kLoop, calls=%fused_computation.43 | loop fusion | flops 2097152 | bytes 6291460 | tf_op jit(solution)/shard_map/mul | solution.py:444
  (37 shorter events, 0.2 us)
Async XLA Ops:
  0.6 1.6 copy-start
  2.3 15.1 %copy-start.4 = (s32[512]{0:T(512)S(1)}, s32[512]{0:T(512)}, u32[]{:S(2)}) copy-start(s32[512]{0:T(512)} %param.27) | copy-start | bytes 6148
  2.3 16.8 %copy-start.6 = (s32[512]{0:T(512)S(1)}, s32[512]{0:T(512)}, u32[]{:S(2)}) copy-start(s32[512]{0:T(512)} %param.23) | copy-start | bytes 6148
  2.3 16.8 %copy-start.7 = (bf16[512]{0:T(512)(128)(2,1)S(1)}, bf16[512]{0:T(512)(128)(2,1)}, u32[]{:S(2)}) copy-start(bf16[512]{0:T(512)(128)(2,1)} %param.22) | copy-start | bytes 3076
  2.3 16.8 %copy-start.8 = (bf16[512]{0:T(512)(128)(2,1)S(1)}, bf16[512]{0:T(512)(128)(2,1)}, u32[]{:S(2)}) copy-start(bf16[512]{0:T(512)(128)(2,1)} %param.21) | copy-start | bytes 3076
  2.3 36.5 %copy-start.9 = (bf16[8]{0:T(256)(128)(2,1)S(1)}, bf16[8]{0:T(256)(128)(2,1)}, u32[]{:S(2)}) copy-start(bf16[8]{0:T(256)(128)(2,1)} %param.25) | copy-start | bytes 52
  2.3 36.5 %copy-start.5 = (s32[512]{0:T(512)S(1)}, s32[512]{0:T(512)}, u32[]{:S(2)}) copy-start(s32[512]{0:T(512)} %param.24) | copy-start | bytes 6148
  7.0 78.0 %copy-start.2 = (f32[2,2048]{1,0:T(2,128)S(1)}, f32[2,2048]{1,0:T(2,128)}, u32[]{:S(2)}) copy-start(f32[2,2048]{1,0:T(2,128)} %param.29) | copy-start | bytes 49156
  7.1 78.0 %copy-start.3 = (f32[2,2048]{1,0:T(2,128)S(1)}, f32[2,2048]{1,0:T(2,128)}, u32[]{:S(2)}) copy-start(f32[2,2048]{1,0:T(2,128)} %param.30) | copy-start | bytes 49156
  23.6 24.5 %all-to-all-start.2 = ((bf16[64,1,16]{2,1,0:T(2,128)(2,1)}), bf16[64,1,16]{2,1,0:T(2,128)(2,1)S(1)}, u32[]{:S(2)}, u32[]{:S(2)}) async-start(bf16[64,1,16]{2,1,0:T(2,128)(2,1)} %all_to_all.21), calls=%async_computation.2 | async-start | bytes 65536 | tf_op jit(solution)/shard_map/all_to_all | solution.py:384
  48.1 14.9 %all-to-all-start.1 = ((bf16[64,1,16]{2,1,0:T(2,128)(2,1)}), bf16[64,1,16]{2,1,0:T(2,128)(2,1)S(1)}, u32[]{:S(2)}, u32[]{:S(2)}) async-start(bf16[64,1,16]{2,1,0:T(2,128)(2,1)} %all_to_all.20), calls=%async_computation.1 | async-start | bytes 65536 | tf_op jit(solution)/shard_map/all_to_all | solution.py:383
  63.0 22.1 %all-to-all-start = ((bf16[64,16,256]{2,1,0:T(8,128)(2,1)}), bf16[64,16,256]{2,1,0:T(8,128)(2,1)S(1)}, u32[]{:S(2)}, u32[]{:S(2)}) async-start(bf16[64,16,256]{2,1,0:T(8,128)(2,1)} %bitcast.11), calls=%async_computation | async-start | bytes 1048576 | tf_op jit(solution)/shard_map/all_to_all | solution.py:382
  87.6 4.6 %copy-start.1 = (f32[2048,1024]{0,1:T(8,128)}, f32[2048,1024]{0,1:T(8,128)S(1)}, u32[]{:S(2)}) copy-start(f32[2048,1024]{0,1:T(8,128)S(1)} %get-tuple-element.198) | copy-start | bytes 25165828 | tf_op jit(solution)/shard_map/while
  112.8 4.6 %copy-start.1 = (f32[2048,1024]{0,1:T(8,128)}, f32[2048,1024]{0,1:T(8,128)S(1)}, u32[]{:S(2)}) copy-start(f32[2048,1024]{0,1:T(8,128)S(1)} %get-tuple-element.198) | copy-start | bytes 25165828 | tf_op jit(solution)/shard_map/while
  138.5 5.2 %collective-permute-start = (f32[2048,256]{1,0:T(8,128)}, f32[2048,256]{1,0:T(8,128)}, u32[]{:S(2)}, u32[]{:S(2)}) collective-permute-start(f32[2048,256]{1,0:T(8,128)} %dynamic-slice_bitcast_fusion), channel_id=1, source_target_pairs={{0,4},{4,0},{8,12},{12,8},{16,20},{20,16},{24,28},{28,24},{32,36},... | collective-permute-start | bytes 6291464 | tf_op jit(solution)/shard_map/ppermute | solution.py:430
  139.0 4.0 %collective-permute-start.1 = (f32[32,128]{1,0:T(8,128)S(1)}, f32[32,128]{1,0:T(8,128)S(1)}, u32[]{:S(2)}, u32[]{:S(2)}) collective-permute-start(f32[32,128]{1,0:T(8,128)S(1)} %fusion.40), channel_id=1, source_target_pairs={{0,4},{4,0},{8,12},{12,8},{16,20},{20,16},{24,28},{28,24},{32,36},... | collective-permute-start | bytes 49160 | tf_op jit(solution)/shard_map/ppermute | solution.py:430

commit v2 on v1

--- a/solution.py
+++ b/solution.py
@@ -79,6 +79,9 @@
             device_id_type=MESH,
         )
 
+    def block_of(yy, zz):
+        return full.at[c, yy * (nz // 2) + zz // 2, :, pl.ds(pl.multiple_of(lax.rem(zz, 2) * 128, 128), 128)]
+
     barrier = pltpu.get_barrier_semaphore()
     for o in range(1, ny):
         pl.semaphore_signal(barrier, inc=1, device_id={"dp": dp_of(yo(o), z)}, device_id_type=MESH)
@@ -159,14 +162,15 @@
     squares = jnp.sum(mine * mine) + jnp.sum(mine_small * mine_small)
     small[c, y, z, :, 0:128] = mine_small
     small[c, y, z, :, 128:256] = jnp.full((1, 128), squares, jnp.float32)
-    full[c, y, z] = mine.astype(jnp.bfloat16)
+    mine_ref = block_of(y, z)
+    mine_ref[...] = mine.T.astype(jnp.bfloat16)
 
     def gz_small(o):
         ref = small.at[c, y, z]
         return copy(ref, ref, gzs_sems, (o - 1,), dp_of(y, zo(o)))
 
     def gz_block(o):
-        ref = full.at[c, y, z]
+        ref = block_of(y, z)
         return copy(ref, ref, gz_sems, (o,), dp_of(y, zo(o)))
 
     def gy_small(o):
@@ -174,11 +178,11 @@
         return copy(ref, ref, gys_sems, (o - 1,), dp_of(yo(o), z))
 
     def gy_block(o, oz):
-        ref = full.at[c, y, zo(nz - oz)]
+        ref = block_of(y, zo(nz - oz))
         return copy(ref, ref, gy_sems, (o - 1, oz), dp_of(yo(o), z))
 
     def pair_block(oy, oz):
-        ref = full.at[c, yo(ny - oy), zo(nz - oz)]
+        ref = block_of(yo(ny - oy), zo(nz - oz))
         return copy(ref, ref, pair_sems, (oy, oz), partner)
 
     for o in range(1, nz):
@@ -284,7 +288,7 @@
     return pl.pallas_call(
         functools.partial(reduce_kernel, ny, nz, nx),
         out_shape=(
-            jax.ShapeDtypeStruct((2, ny, nz, rows, width), bf16),
+            jax.ShapeDtypeStruct((2, ny * nz // 2, 128, 256), bf16),
             jax.ShapeDtypeStruct((2, ny, nz, 1, 256), f32),
             jax.ShapeDtypeStruct((1, 128), f32),
         ),
@@ -317,6 +321,498 @@
     )(h, hs)
 
 
+def dot_nt(a, b):
+    return lax.dot_general(a, b, (((1,), (1,)), ((), ())), preferred_element_type=jnp.float32)
+
+
+def dot_nn(a, b):
+    return lax.dot_general(a, b, (((1,), (0,)), ((), ())), preferred_element_type=jnp.float32)
+
+
+def dot_tn(a, b):
+    return lax.dot_general(a, b, (((0,), (0,)), ((), ())), preferred_element_type=jnp.float32)
+
+
+def iota(shape, axis):
+    return lax.broadcasted_iota(jnp.int32, shape, axis)
+
+
+def ones_where(mask):
+    return jnp.where(mask, 1.0, 0.0).astype(jnp.bfloat16)
+
+
+def dispatch_kernel(
+    ny,
+    nz,
+    nx,
+    cap,
+    features,
+    next_features,
+    ints,
+    reals,
+    source_weight,
+    target_w1,
+    target_mean,
+    target_scale,
+    target_shift,
+    target_head,
+    rows,
+    notes,
+    sent,
+    sent_notes,
+    q_all,
+    acc,
+    row_sems,
+    note_sems,
+    pair_sems,
+    pair_note,
+    q_sems,
+):
+    f32, bf16 = jnp.float32, jnp.bfloat16
+    shards = 2 * ny * nz
+    tokens = features.shape[0]
+    me = lax.axis_index("dp")
+    mx = lax.axis_index("member")
+    c = lax.rem(me, 2)
+    z = lax.rem(me // 2, nz)
+    y = me // (2 * nz)
+    partner = me + 1 - 2 * c
+
+    def peer(i, sign):
+        oc = lax.rem(i, 2)
+        oz = lax.rem(far_first(lax.rem(i // 2, nz), nz), nz)
+        oy = i // (2 * nz)
+        yy = lax.rem(y + ny + sign * oy, ny)
+        zz = lax.rem(z + nz + sign * oz, nz)
+        return (yy * nz + zz) * 2 + lax.rem(c + oc, 2)
+
+    last = 2 * nz - 2
+
+    def step_of(i):
+        return i + jnp.where(i >= last, 1, 0)
+
+    def remote(src, dst, send, recv, device):
+        return pltpu.make_async_remote_copy(
+            src_ref=src, dst_ref=dst, send_sem=send, recv_sem=recv, device_id=device, device_id_type=MESH
+        )
+
+    barrier = pltpu.get_barrier_semaphore()
+
+    def greet(i, _):
+        pl.semaphore_signal(
+            barrier, inc=1, device_id={"dp": peer(step_of(i), 1)}, device_id_type=MESH
+        )
+        return 0
+
+    lax.fori_loop(0, shards - 1, greet, 0)
+    for o in range(1, nx):
+        pl.semaphore_signal(
+            barrier, inc=1, device_id={"member": lax.rem(mx + o, nx)}, device_id_type=MESH
+        )
+
+    dest = ints[4:5, :]
+    to_shard = dest == iota((shards, tokens), 0)
+    chosen = ones_where(to_shard)
+    before = ones_where(iota((tokens, tokens), 0) < iota((tokens, tokens), 1))
+    rank = jnp.sum(jnp.where(to_shard, dot_nn(chosen, before), 0.0), axis=0, keepdims=True)
+    rank = rank.astype(jnp.int32)
+    slot = dest * cap + rank
+    chunk = min(16, shards) * cap
+    per = min(16, shards)
+
+    def place(i, _):
+        pick = ones_where(iota((chunk, tokens), 0) + i * chunk == slot)
+        block = dot_nn(pick, features[...]).astype(bf16)
+        sent[pl.ds(i * per, per)] = block.reshape(per, cap, features.shape[1])
+        return 0
+
+    lax.fori_loop(0, shards // per, place, 0)
+    weight = jnp.zeros((1, tokens), f32)
+    for k in range(source_weight.shape[0]):
+        weight = jnp.where(ints[1:2, :] == k, source_weight[k], weight)
+
+    pl.semaphore_wait(barrier, shards + nx - 2)
+
+    def row_copy(i):
+        to = peer(i, 1)
+        return remote(
+            sent.at[to], rows.at[lax.rem(to, 2), me], row_sems.at[0, i], row_sems.at[1, i], {"dp": to}
+        )
+
+    def row_landed(i):
+        ref = rows.at[c, peer(i, -1)]
+        return remote(ref, ref, row_sems.at[0, i], row_sems.at[1, i], {"dp": peer(i, 1)})
+
+    def send_rows(i, _):
+        row_copy(step_of(i)).start()
+        return 0
+
+    lax.fori_loop(0, shards - 1, send_rows, 0)
+    rows[c, me] = sent[me]
+
+    hidden = target_w1.shape[1]
+    wide = min(256, hidden)
+    tall = 128 if tokens % 128 == 0 else tokens
+    acc[...] = jnp.zeros(acc.shape, f32)
+    for k in range(2):
+
+        def block(i, _, k=k):
+            units = pl.ds(pl.multiple_of(i * wide, wide), wide)
+            scale = target_scale[k : k + 1, units]
+            shift = target_shift[k : k + 1, units] - target_mean[k : k + 1, units] * scale
+            head = target_head[k : k + 1, units]
+            w = target_w1[k, units, :]
+            for t in range(tokens // tall):
+                pre = dot_nt(next_features[t * tall : (t + 1) * tall, :], w)
+                term = jnp.maximum(pre * scale + shift, 0.0) * head
+                total = term[:, 0:128]
+                for part in range(1, wide // 128):
+                    total = total + term[:, part * 128 : (part + 1) * 128]
+                acc[k, t * tall : (t + 1) * tall, :] += total
+            return 0
+
+        lax.fori_loop(0, hidden // wide, block, 0)
+    for k in range(2):
+        q_all[mx, k] = jnp.sum(acc[k].T, axis=0, keepdims=True)
+
+    def q_copy(o):
+        ref = q_all.at[mx]
+        return remote(ref, ref, q_sems.at[0, o - 1], q_sems.at[1, o - 1], {"member": lax.rem(mx + o, nx)})
+
+    for o in range(1, nx):
+        q_copy(o).start()
+    for o in range(1, nx):
+        q_copy(o).wait_recv()
+    first = jnp.zeros((1, tokens), f32)
+    second = first
+    for k in range(2 * nx):
+        value = q_all[k // 2, k % 2]
+        first = jnp.where(ints[2:3, :] == k, value, first)
+        second = jnp.where(ints[3:4, :] == k, value, second)
+    lowest = jnp.minimum(first, second)
+    carry = 1.0 - ints[0:1, :].astype(f32)
+    target = reals[0:1, :] + GAMMA * carry * (lowest - ALPHA * reals[1:2, :])
+
+    lane = iota((128, tokens), 0)
+    spread = jnp.where(to_shard, target, 0.0).astype(bf16)
+    spread_w = jnp.where(to_shard, weight, 0.0).astype(bf16)
+    note = dot_nt(spread, ones_where(lane == rank)) + dot_nt(
+        spread_w, ones_where(lane == rank + cap)
+    )
+    sent_notes[...] = note.reshape(shards, 1, 128)
+
+    def note_copy(i):
+        to = peer(i, 1)
+        return remote(
+            sent_notes.at[to],
+            notes.at[lax.rem(to, 2), me],
+            note_sems.at[0, i],
+            note_sems.at[1, i],
+            {"dp": to},
+        )
+
+    def note_landed(i):
+        ref = notes.at[c, peer(i, -1)]
+        return remote(ref, ref, note_sems.at[0, i], note_sems.at[1, i], {"dp": peer(i, 1)})
+
+    def send_notes(i, _):
+        note_copy(step_of(i)).start()
+        return 0
+
+    lax.fori_loop(0, shards - 1, send_notes, 0)
+    notes[c, me] = sent_notes[me]
+
+    def pair_copy(i):
+        ref = rows.at[c, peer(i, -1)]
+        return remote(ref, ref, pair_sems.at[0, i], pair_sems.at[1, i], {"dp": partner})
+
+    pair_copy(last).start()
+
+    def relay(i, _):
+        step = step_of(shards - 2 - i)
+        row_landed(step).wait_recv()
+        pair_copy(step).start()
+        return 0
+
+    lax.fori_loop(0, shards - 1, relay, 0)
+
+    def note_wait(i, _):
+        note_landed(step_of(i)).wait_recv()
+        return 0
+
+    lax.fori_loop(0, shards - 1, note_wait, 0)
+    pair_n = remote(notes.at[c], notes.at[c], pair_note.at[0], pair_note.at[1], {"dp": partner})
+    pair_n.start()
+
+    def drain(i, _):
+        row_copy(step_of(i)).wait_send()
+        note_copy(step_of(i)).wait_send()
+        return 0
+
+    lax.fori_loop(0, shards - 1, drain, 0)
+
+    def pair_wait(i, _):
+        pair_copy(i).wait()
+        return 0
+
+    lax.fori_loop(0, shards, pair_wait, 0)
+    for o in range(1, nx):
+        q_copy(o).wait_send()
+    pair_n.wait()
+
+
+def dispatch(features, next_features, ints, reals, source_weight, targets, ny, nz, nx):
+    tokens, width = features.shape
+    shards = 2 * ny * nz
+    cap = 2 * tokens // shards
+    f32, bf16 = jnp.float32, jnp.bfloat16
+    vmem = pl.BlockSpec(memory_space=pltpu.VMEM)
+    dma = pltpu.SemaphoreType.DMA
+    return pl.pallas_call(
+        functools.partial(dispatch_kernel, ny, nz, nx, cap),
+        out_shape=(
+            jax.ShapeDtypeStruct((2, shards, cap, width), bf16),
+            jax.ShapeDtypeStruct((2, shards, 1, 128), f32),
+        ),
+        in_specs=[vmem] * 4 + [pl.BlockSpec(memory_space=pltpu.SMEM)] + [vmem] * 5,
+        out_specs=[vmem] * 2,
+        scratch_shapes=[
+            pltpu.VMEM((shards, cap, width), bf16),
+            pltpu.VMEM((shards, 1, 128), f32),
+            pltpu.VMEM((nx, 2, 1, tokens), f32),
+            pltpu.VMEM((2, tokens, 128), f32),
+            dma((2, shards)),
+            dma((2, shards)),
+            dma((2, shards)),
+            dma((2,)),
+            dma((2, nx - 1)),
+        ],
+        compiler_params=pltpu.CompilerParams(collective_id=1, has_side_effects=True),
+        cost_estimate=pl.CostEstimate(flops=10**9, bytes_accessed=4 * 10**6, transcendentals=0),
+        name="dispatch",
+    )(features, next_features, ints, reals, source_weight, *targets)
+
+
+def critic_kernel(
+    cap,
+    tile,
+    rows,
+    notes,
+    shift_all,
+    head_all,
+    w_hbm,
+    h,
+    hs,
+    w_wide,
+    w,
+    xc,
+    targets,
+    weights,
+    zbuf,
+    gbuf,
+    gz,
+    gt,
+    sq,
+    s0,
+    s1,
+    sem,
+):
+    f32, bf16 = jnp.float32, jnp.bfloat16
+    slots, width = rows.shape[1:]
+    hidden = w.shape[0]
+    shards = slots // cap
+    pieces = slots // 128
+    few, many = 3, 6
+    wide = min(256, hidden)
+    lanes = hidden // 128
+    c = lax.rem(lax.axis_index("dp"), 2)
+    fetch = pltpu.make_async_copy(w_hbm.at[c], w_wide, sem)
+    fetch.start()
+    shift = shift_all[pl.ds(c, 1), :]
+    head = head_all[pl.ds(c, 1), :]
+
+    owner = ones_where(iota((shards, slots), 1) // cap == iota((shards, slots), 0))
+    my_slot = lax.rem(iota((cap, slots), 1), cap) == iota((cap, slots), 0)
+    upto = ones_where(iota((128, 128), 0) <= iota((128, 128), 1))
+    counts = []
+    for s in range(2):
+        by_slot = notes[s, :, 0, :].T[0 : 2 * cap].astype(bf16)
+        spread = dot_nn(by_slot, owner)
+        y_row = jnp.sum(jnp.where(my_slot, spread[0:cap], 0.0), axis=0, keepdims=True)
+        w_row = jnp.sum(jnp.where(my_slot, spread[cap : 2 * cap], 0.0), axis=0, keepdims=True)
+        alive = jnp.where(w_row > 0, 1.0, 0.0)
+        stacked = jnp.concatenate(
+            [alive[:, p * 128 : (p + 1) * 128] for p in range(pieces)]
+            + [jnp.zeros((8, 128), f32)] * (1 if pieces < 8 else 0),
+            axis=0,
+        )
+        running = dot_nn(stacked.astype(bf16), upto)
+        place = []
+        start = jnp.zeros((1, 1), f32)
+        for p in range(pieces):
+            position = running[p : p + 1] - 1.0 + start
+            position = jnp.where(stacked[p : p + 1] > 0, position, -1.0)
+            place.append(position.astype(jnp.int32))
+            start = start + running[p : p + 1, 127:128]
+        number = jnp.sum(alive)
+        counts.append(number)
+        y_wide = jnp.broadcast_to(y_row, (128, slots)).astype(bf16)
+        w_wide_row = jnp.broadcast_to(w_row, (128, slots)).astype(bf16)
+        trips = jnp.where(number <= few * tile, few, many)
+
+        def compact(i, _, s=s, place=place, y_wide=y_wide, w_wide_row=w_wide_row):
+            at = pl.ds(pl.multiple_of(i * tile, tile), tile)
+            row = iota((tile, 128), 0) + i * tile
+            pick = jnp.concatenate([ones_where(row == p) for p in place], axis=1)
+            xc[s, at, :] = dot_nn(pick, rows[s]).astype(bf16)
+            targets[s, at, :] = dot_nt(pick, y_wide)
+            weights[s, at, :] = dot_nt(pick, w_wide_row)
+            return 0
+
+        lax.fori_loop(0, trips, compact, 0)
+
+    fetch.wait()
+    w[...] = w_wide[...].astype(bf16)
+    total0 = jnp.zeros((1, hidden), f32)
+    total1 = jnp.zeros((1, hidden), f32)
+    groups = tile // 8
+    for s in range(2):
+        number = counts[s]
+        whole = jnp.full((1, 1), number, f32)
+        trips = jnp.where(number <= few * tile, few, many)
+        middle = jnp.sum(rows[s].astype(f32), axis=0, keepdims=True) / whole
+        one = middle.astype(bf16)
+        rest = middle - one.astype(f32)
+        two = rest.astype(bf16)
+        three = (rest - two.astype(f32)).astype(bf16)
+        parts = jnp.concatenate(
+            [one.astype(f32), two.astype(f32), three.astype(f32), jnp.zeros((13, width), f32)], axis=0
+        ).astype(bf16)
+        mu = jnp.sum(dot_nt(parts, w[...]), axis=0, keepdims=True)
+        sq[...] = jnp.zeros(sq.shape, f32)
+        s0[...] = jnp.zeros(s0.shape, f32)
+        s1[...] = jnp.zeros(s1.shape, f32)
+
+        def forward(i, _, s=s, mu=mu, number=number):
+            at = pl.ds(pl.multiple_of(i * tile, tile), tile)
+            row = iota((tile, 128), 0) + i * tile
+            alive = jnp.where(row < number.astype(jnp.int32), 1.0, 0.0)
+            x = xc[s, at, :]
+            for j in range(hidden // wide):
+                pre = dot_nt(x, w[j * wide : (j + 1) * wide, :])
+                for k in range(wide // 128):
+                    lo = j * wide + k * 128
+                    zc = (pre[:, k * 128 : (k + 1) * 128] - mu[:, lo : lo + 128]) * alive
+                    zbuf[at, lo : lo + 128] = zc
+                    sq[:, lo : lo + 128] += jnp.sum((zc * zc).reshape(groups, 8, 128), axis=0)
+            return 0
+
+        lax.fori_loop(0, trips, forward, 0)
+        var = jnp.sum(sq[...], axis=0, keepdims=True) / whole
+        inv = 1.0 / jnp.sqrt(var + EPS)
+
+        def slopes(i, _, s=s, inv=inv):
+            at = pl.ds(pl.multiple_of(i * tile, tile), tile)
+            acc = jnp.zeros((tile, 128), f32)
+            for j in range(lanes):
+                cut = slice(j * 128, (j + 1) * 128)
+                zh = zbuf[at, cut] * inv[:, cut]
+                zbuf[at, cut] = zh
+                acc = acc + jnp.maximum(zh + shift[:, cut], 0.0) * head[:, cut]
+            q = jnp.sum(acc, axis=1, keepdims=True)
+            dq = weights[s, at, :] * (q - targets[s, at, :])
+            for j in range(lanes):
+                cut = slice(j * 128, (j + 1) * 128)
+                zh = zbuf[at, cut]
+                g = jnp.where(zh > -shift[:, cut], dq, 0.0)
+                gbuf[at, cut] = g
+                s0[:, cut] += jnp.sum(g.reshape(groups, 8, 128), axis=0)
+                s1[:, cut] += jnp.sum((g * zh).reshape(groups, 8, 128), axis=0)
+            return 0
+
+        lax.fori_loop(0, trips, slopes, 0)
+        sum0 = jnp.sum(s0[...], axis=0, keepdims=True)
+        sum1 = jnp.sum(s1[...], axis=0, keepdims=True)
+        total0 = total0 + sum0
+        total1 = total1 + sum1
+        scale = inv * head
+        base = -scale * (sum0 / whole)
+        tilt = -scale * (sum1 / whole)
+
+        def backward(i, _, scale=scale, base=base, tilt=tilt):
+            at = pl.ds(pl.multiple_of(i * tile, tile), tile)
+            for j in range(lanes):
+                cut = slice(j * 128, (j + 1) * 128)
+                value = gbuf[at, cut] * scale[:, cut] + (zbuf[at, cut] * tilt[:, cut] + base[:, cut])
+                gz[at, cut] = value.astype(bf16)
+            return 0
+
+        lax.fori_loop(0, trips, backward, 0)
+
+        def product(depth, s=s):
+            x = xc[s, 0:depth, :]
+            for j in range(hidden // wide):
+                cut = slice(j * wide, (j + 1) * wide)
+                out = dot_tn(x, gz[0:depth, cut])
+                gt[:, cut] = out if s == 0 else gt[:, cut] + out
+
+        @pl.when(trips == few)
+        def _():
+            product(few * tile)
+
+        @pl.when(trips != few)
+        def _():
+            product(many * tile)
+
+    g_shift = head * total0
+    g_head = shift * total0 + total1
+    for u in range(lanes):
+        cut = slice(u * 128, (u + 1) * 128)
+        h[2 * u] = gt[0:128, cut].astype(bf16)
+        h[2 * u + 1] = gt[128:256, cut].astype(bf16)
+        hs[2 * u] = g_shift[:, cut]
+        hs[2 * u + 1] = g_head[:, cut]
+
+
+def critic_sums(rows, notes, shift, head, w1, cap):
+    f32, bf16 = jnp.float32, jnp.bfloat16
+    slots, width = rows.shape[1:]
+    hidden = w1.shape[1]
+    tile = slots * 3 // 16
+    tall = 6 * tile
+    vmem = pl.BlockSpec(memory_space=pltpu.VMEM)
+    blocks = hidden // 128 * (width // 128)
+    return pl.pallas_call(
+        functools.partial(critic_kernel, cap, tile),
+        out_shape=(
+            jax.ShapeDtypeStruct((blocks, 128, 128), bf16),
+            jax.ShapeDtypeStruct((blocks, 1, 128), f32),
+        ),
+        in_specs=[vmem] * 4 + [pl.BlockSpec(memory_space=pl.ANY)],
+        out_specs=[vmem] * 2,
+        scratch_shapes=[
+            pltpu.VMEM((hidden, width), f32),
+            pltpu.VMEM((hidden, width), bf16),
+            pltpu.VMEM((2, tall, width), bf16),
+            pltpu.VMEM((2, tall, 128), f32),
+            pltpu.VMEM((2, tall, 128), f32),
+            pltpu.VMEM((tall, hidden), f32),
+            pltpu.VMEM((tall, hidden), f32),
+            pltpu.VMEM((tall, hidden), bf16),
+            pltpu.VMEM((width, hidden), f32),
+            pltpu.VMEM((8, hidden), f32),
+            pltpu.VMEM((8, hidden), f32),
+            pltpu.VMEM((8, hidden), f32),
+            pltpu.SemaphoreType.DMA,
+        ],
+        compiler_params=pltpu.CompilerParams(vmem_limit_bytes=60 * 2**20),
+        cost_estimate=pl.CostEstimate(
+            flops=8 * slots * hidden * width, bytes_accessed=4 * 10**6, transcendentals=0
+        ),
+        name="critic_sums",
+    )(rows, notes, shift, head, w1)
+
+
 def per_device(
     features,
     next_features,
@@ -336,115 +832,43 @@
     target_shift,
     target_head,
 ):
+    f32 = jnp.float32
     shards = lax.axis_size("dp")
-    members = lax.axis_size("member")
-    local_rows = features.shape[0]
-    width = features.shape[1]
-    local_critics = critic_w1.shape[0]
-    total_critics = local_critics * members
-    capacity = 2 * local_rows // shards
-    slot_total = shards * capacity
-    shard_iota = jnp.arange(shards, dtype=jnp.int32)
-    picked = (destination[:, None] == shard_iota[None]).astype(jnp.int32)
-    earlier = jnp.cumsum(picked, axis=0) - picked
-    rank = jnp.sum(earlier * picked, axis=1)
-    position = destination * capacity + rank
-
-    def place(values):
-        empty = jnp.zeros((slot_total,) + values.shape[1:], values.dtype)
-        return empty.at[position].set(values).reshape((shards, capacity) + values.shape[1:])
-
-    source_iota = jnp.arange(source_weight.shape[0], dtype=jnp.int32)
-    weight_rows = jnp.sum(
-        jnp.where(
-            source_ids[:, None] == source_iota[None], source_weight.astype(jnp.float32)[None], 0.0
-        ),
-        axis=1,
-    ).astype(jnp.bfloat16)
-    carry_rows = (1 - terminal).astype(jnp.bfloat16)
-    pre_act = jnp.einsum(
-        "si,cfi->csf", next_features, target_w1, preferred_element_type=jnp.float32
-    )
-    active = jnp.maximum(
-        (pre_act - target_mean[:, None]) * target_scale[:, None] + target_shift[:, None], 0.0
-    )
-    mine = jnp.sum(active * target_head[:, None], axis=2).T
-    everyone = lax.all_gather(mine, "member", axis=1, tiled=True)
-    critic_iota = jnp.arange(total_critics, dtype=jnp.int32)
-    first = jnp.sum(jnp.where(subset[:, 0][:, None] == critic_iota[None], everyone, 0.0), axis=1)
-    second = jnp.sum(jnp.where(subset[:, 1][:, None] == critic_iota[None], everyone, 0.0), axis=1)
-    lowest = jnp.minimum(first, second)
-    value = rewards.astype(jnp.float32) + GAMMA * carry_rows.astype(jnp.float32) * (
-        lowest - ALPHA * next_logp.astype(jnp.float32)
-    )
-    value = value.astype(jnp.bfloat16)
-    received, weight_slots, target_slots = (
-        lax.all_to_all(place(features), "dp", split_axis=0, concat_axis=0, tiled=True),
-        lax.all_to_all(place(weight_rows), "dp", split_axis=0, concat_axis=0, tiled=True),
-        lax.all_to_all(place(value), "dp", split_axis=0, concat_axis=0, tiled=True),
-    )
-    rows_in = received.reshape(slot_total, width)
-    weight = weight_slots.reshape(slot_total).astype(jnp.float32)
-    target = target_slots.reshape(slot_total).astype(jnp.float32)
-    live = (weight > 0).astype(jnp.float32)
-    live_count = jnp.sum(live)
-    live_col = live[:, None]
-
-    def critic(params):
-        weights, offset, output = params
-        pre_act = jnp.dot(
-            rows_in, weights.astype(jnp.bfloat16).T, preferred_element_type=jnp.float32
-        )
-        centred = pre_act - jnp.sum(pre_act * live_col, axis=0, keepdims=True) / live_count
-        inverse = 1.0 / jnp.sqrt(
-            jnp.sum(centred * centred * live_col, axis=0, keepdims=True) / live_count + EPS
-        )
-        normed = centred * inverse
-        before = normed + offset[None]
-        active = jnp.maximum(before, 0.0)
-        value_now = jnp.sum(active * output[None], axis=1)
-        slope = weight * (value_now - target)
-        grad_head = jnp.dot(slope, active)
-        grad_unit = jnp.where(before > 0, slope[:, None] * output[None], 0.0)
-        grad_shift = jnp.sum(grad_unit, axis=0)
-        unit_mean = jnp.sum(grad_unit * live_col, axis=0, keepdims=True) / live_count
-        cross_mean = jnp.sum(grad_unit * normed * live_col, axis=0, keepdims=True) / live_count
-        grad_pre = (inverse * (grad_unit - unit_mean - normed * cross_mean) * live_col).astype(
-            jnp.bfloat16
-        )
-        grad_w1 = jnp.dot(grad_pre.T, rows_in, preferred_element_type=jnp.float32)
-        return (grad_w1, grad_shift, grad_head)
-
-    grad_w1, grad_shift, grad_head = lax.map(critic, (critic_w1, critic_shift, critic_head))
-    hidden = critic_w1.shape[1]
-    root = jnp.float32(math.sqrt(total_critics * hidden * (width + 2)))
+    nx = lax.axis_size("member")
     nz = NZ
     ny = shards // (2 * nz)
-    blocks = ny * nz
-    core = lax.rem(lax.axis_index("dp"), 2)
-    pairs = [(i, i ^ 1) for i in range(shards)]
-
-    def half_sum(a):
-        keep = lax.dynamic_index_in_dim(a, core, 0, keepdims=False)
-        give = lax.dynamic_index_in_dim(a, 1 - core, 0, keepdims=False)
-        return keep + lax.ppermute(give, "dp", pairs)
-
-    h = half_sum(grad_w1).astype(jnp.bfloat16).reshape(ny, nz, hidden // blocks, width)
-    vectors = jnp.concatenate(
-        [
-            grad_shift.reshape(2, blocks, hidden // blocks),
-            grad_head.reshape(2, blocks, hidden // blocks),
-        ],
-        axis=2,
+    tokens, width = features.shape
+    critics, hidden = critic_w1.shape[:2]
+    cap = 2 * tokens // shards
+    zero = jnp.zeros_like(terminal)
+    ints = jnp.stack(
+        [terminal, source_ids, subset[:, 0], subset[:, 1], destination, zero, zero, zero]
     )
-    hs = half_sum(vectors).reshape(ny, nz, 1, 2 * hidden // blocks)
-    full, small, squares = reduce_all(h, hs, ny, nz, members)
+    reals = jnp.stack([rewards, next_logp]).astype(f32)
+    rows, notes = dispatch(
+        features,
+        next_features,
+        ints,
+        reals,
+        source_weight.astype(f32),
+        (target_w1, target_mean, target_scale, target_shift, target_head),
+        ny,
+        nz,
+        nx,
+    )
+    h, hs = critic_sums(
+        rows.reshape(2, shards * cap, width), notes, critic_shift, critic_head, critic_w1, cap
+    )
+    h = h.reshape(ny, nz, 128, 128)
+    hs = hs.reshape(ny, nz, 1, 128)
+    full, small, squares = reduce_all(h, hs, ny, nz, nx)
+    root = jnp.float32(math.sqrt(critics * nx * hidden * (width + 2)))
     norm = jnp.sqrt(squares[0, 0])
     factor = root / jnp.maximum(norm, root)
-    step_w1 = full.reshape(2, hidden, width).astype(jnp.float32) * factor
-    per = hidden // blocks
-    step_shift = small[..., 0, 0:per].reshape(2, hidden) * factor
-    step_head = small[..., 0, per : 2 * per].reshape(2, hidden) * factor
+    step_w1 = full.reshape(critics, hidden, width).astype(f32) * factor
+    small = small[..., 0, 0:128].reshape(critics, hidden // 128, 2, 128)
+    step_shift = small[:, :, 0, :].reshape(critics, hidden) * factor
+    step_head = small[:, :, 1, :].reshape(critics, hidden) * factor
     return (step_w1, step_shift, step_head)
 
 

time: 203 us -> 117 us (0.58)
  Pallas kernels: 47.3 us -> 105 us
  other arithmetic: 41.4 us -> 5.99 us
  matrix products: 28.9 us -> 0 us
  starting transfers between devices: 26.3 us -> 0 us
  waiting for transfers between devices: 26.3 us -> 0 us
  local copies, waits for them, and re-layouts: 19.5 us -> 4.86 us
  blocking collectives: 10.3 us -> 0 us
    pallas_call x0 -> x2, Pallas kernels: none -> 56.9 us  [the longest x1 38 us: dispatch(): pl.pallas_call(functools.partial(dispatch_kernel, ny, nz, nx, cap), out_s...]
    dot_general x7 -> x0, matrix products: 28.9 us -> none  [the longest x2 16.4 us: critic(): grad_w1 = jnp.dot(grad_pre.T, rows_in, preferred_element_type=jnp.float32)]
    all_to_all x3 -> x0, starting transfers between devices: 25.6 us -> none  [the longest x1 15.2 us: per_device(): lax.all_to_all(place(value), 'dp', split_axis=0, concat_axis=0, tiled=True)]
    all_to_all x3 -> x0, waiting for transfers between devices: 22.8 us -> none  [the longest x1 12.4 us: per_device(): lax.all_to_all(place(features), 'dp', split_axis=0, concat_axis=0, tiled=...]
    reduce_sum x9 -> x0, other arithmetic: 22 us -> none  [the longest x2 15.4 us: critic(): jnp.sum(grad_unit * live_col, axis=0, keepdims=True) / live_count]
    scatter x3 -> x0, local copies, waits for them, and re-layouts: 11.1 us -> none  [place(): empty.at[position].set(values)]
    all_gather x1 -> x0, blocking collectives: 10.3 us -> none  [per_device(): everyone = lax.all_gather(mine, 'member', axis=1, tiled=True)]
    unnamed x1 -> x0, other arithmetic: 3.79 us -> none
  transfers between devices with their start and end apart: 5 -> 0, of which waited for: 4 -> 0; matrix products, arithmetic and copies ran while one was open for 7% -> 0% of each run, Pallas kernels for 0% -> 0%
where the time goes in v2:
time: 117 us
  Pallas kernels  105 us (90%)
  other arithmetic  5.99 us (5%)
  local copies, waits for them, and re-layouts  4.86 us (4%)
  between operations  1.37 us (1%)
    pallas_call x1, Pallas kernels, reduce_all(): pl.pallas_call(functools.partial(reduce_kernel, ny, nz, nx), out_shape=(j...  47.6 us
    pallas_call x1, Pallas kernels, dispatch(): pl.pallas_call(functools.partial(dispatch_kernel, ny, nz, nx, cap), out_s...  38 us
    pallas_call x1, Pallas kernels, critic_sums(): pl.pallas_call(functools.partial(critic_kernel, cap, tile), out_shape=(ja...  19 us
    mul x1, other arithmetic, per_device(): step_w1 = full.reshape(critics, hidden, width).astype(f32) * factor  4.13 us

profile of v2, /device:TPU:1, one launch (start us, length us, event | category | flops | bytes accessed | tf_op | source)
XLA Modules:
  0.0 116.8 jit_solution(16845143220685942374)
XLA Ops:
  0.6 1.2 convert_element_type.11.source_weight
  1.8 0.7 stack.29
  2.5 0.7 stack.30
  3.2 0.6 maximum_convert_fusion.reals
  3.8 0.8 slice_bitcast_fusion
  4.5 1.3 %stack.28.ints = s32[8,512]{1,0:T(8,128)} concatenate(s32[1,512]{1,0:T(1,128)} %bitcast.26, s32[1,512]{1,0:T(1,128)} %bitcast.27, s32[1,512]{1,0:T(1,128)S(1)} %get-tuple-element.20, s32[1,512]{1,0:T(1,128)S(1)} %get-tuple-element.19, s32[1,512]{1,0:T(1,128)} %bitcast.28, s32[1,512]{1,0:T(1,128)S(1)} %stack_broadcast_in_dim.3, s32[2,512]{1,0:T(2,128)S(1)} %stack.27), dimensions={0} | concatenate | bytes 32768 | tf_op jit(solution)/shard_map/stack | solution.py:844
  5.9 38.0 %dispatch.1 = (bf16[2,64,16,256]{3,2,1,0:T(8,128)(2,1)}, f32[2,64,1,128]{3,2,1,0:T(1,128)}) custom-call(bf16[512,256]{1,0:T(8,128)(2,1)} %features.1, bf16[512,256]{1,0:T(8,128)(2,1)} %next_features.1, s32[8,512]{1,0:T(8,128)} %stack.28.ints, f32[2,512]{1,0:T(2,128)} %maximum_convert_fusion.reals, f32[8]{0:T(128)} %convert_element_type.11.source_weight, ...), custom_call_target="tpu_custom_call" | custom-call | flops 1000000000 | bytes 4000000 | tf_op jit(solution)/shard_map/dispatch/pallas_call | solution.py:571
  43.9 19.0 %critic_sums.1 = (bf16[32,128,128]{2,1,0:T(8,128)(2,1)}, f32[32,1,128]{2,1,0:T(1,128)}) custom-call(bf16[2,1024,256]{2,1,0:T(8,128)(2,1)} %bitcast.30, f32[2,64,1,128]{3,2,1,0:T(1,128)} %get-tuple-element.11.notes, f32[2,2048]{1,0:T(2,128)} %shift_all.1, f32[2,2048]{1,0:T(2,128)} %head_all.1, f32[2,2048,256]{2,1,0:T(8,128)} %w_hbm.1), custom_call_target="tpu_custom_call" | custom-call | flops 4294967296 | bytes 4000000 | tf_op jit(solution)/shard_map/critic_sums/pallas_call | solution.py:785
  62.8 47.6 %gradient_sum.1 = (bf16[2,16,128,256]{3,2,1,0:T(8,128)(2,1)}, f32[2,4,8,1,256]{4,3,2,1,0:T(1,128)}, f32[1,128]{1,0:T(1,128)}) custom-call(bf16[4,8,128,128]{3,2,1,0:T(8,128)(2,1)} %bitcast.21, f32[4,8,1,128]{3,2,1,0:T(1,128)} %bitcast.25), custom_call_target="tpu_custom_call" | custom-call | flops 10000000 | bytes 4000000 | tf_op jit(solution)/shard_map/gradient_sum/pallas_call | solution.py:288
  111.2 0.8 slice.21
  111.9 0.1 fusion
  112.0 0.6 copy_bitcast_fusion
  112.6 4.1 %convert_multiply_fusion = f32[2,16,128,256]{3,2,1,0:T(8,128)} fusion(bf16[2,16,128,256]{3,2,1,0:T(8,128)(2,1)} %get-tuple-element.14, f32[]{:T(128)} %bitcast.8), kind=kLoop, calls=%fused_computation | loop fusion | flops 2097152 | bytes 6291460 | tf_op jit(solution)/shard_map/mul | solution.py:868
  (2 shorter events, 0.0 us)

commit v3 on v2

v3 whole, which is shorter than its diff:
```python
import functools
import math

import jax
import jax.numpy as jnp
from jax import lax
from jax.experimental import pallas as pl
from jax.experimental.pallas import tpu as pltpu
from jax.sharding import PartitionSpec as P

GAMMA = 0.99
ALPHA = 0.2
EPS = 1e-05
NZ = 8
MESH = pl.DeviceIdType.MESH


def far_first(i, nz):
    half = nz // 2
    return half + ((i + 1) // 2) * (2 * ((i + 1) % 2) - 1)


def reduce_kernel(
    ny,
    nz,
    nx,
    h,
    hs,
    full,
    shift_out,
    head_out,
    factor_out,
    t_in,
    m_out,
    n_in,
    r_out,
    r_in,
    small,
    ys_in,
    zs_out,
    zs_in,
    x_out,
    x_in,
    t_sems,
    u_sems,
    m_sems,
    r_sems,
    gz_sems,
    tie_sems,
    gy_sems,
    go_sems,
    pair_sems,
    ys_sems,
    zs_sems,
    gzs_sems,
    gys_sems,
    pair_small,
    x_sems,
):
    f32, bf16 = jnp.float32, jnp.bfloat16
    me = lax.axis_index("dp")
    mx = lax.axis_index("member")
    c = lax.rem(me, 2)
    z = lax.rem(me // 2, nz)
    y = me // (2 * nz)
    partner = me + 1 - 2 * c
    half = nz // 2
    started = []

    def dp_of(yy, zz):
        return (yy * nz + zz) * 2 + c

    def yo(o):
        return lax.rem(y + (o % ny), ny)

    def zo(o):
        return lax.rem(z + (o % nz), nz)

    up, down, over = yo(1), yo(-1), yo(2)

    def copy(src, dst, sems, index, device):
        return pltpu.make_async_remote_copy(
            src_ref=src,
            dst_ref=dst,
            send_sem=sems.at[(0,) + index],
            recv_sem=sems.at[(1,) + index],
            device_id=device,
            device_id_type=MESH,
        )

    def send(*args):
        c = copy(*args)
        c.start()
        started.append(c)

    def landed(ref, sems, index):
        copy(ref, ref, sems, index, {"dp": partner}).wait_recv()

    def to_y(yy):
        return {"dp": dp_of(yy, z)}

    def to_z(zz):
        return {"dp": dp_of(y, zz)}

    def block_of(yy, zz):
        return full.at[
            c, yy * (nz // 2) + zz // 2, :, pl.ds(pl.multiple_of(lax.rem(zz, 2) * 128, 128), 128)
        ]

    def half_of(yy, zz, part):
        return full.at[
            c,
            yy * (nz // 2) + zz // 2,
            pl.ds(part * 64, 64),
            pl.ds(pl.multiple_of(lax.rem(zz, 2) * 128, 128), 128),
        ]

    barrier = pltpu.get_barrier_semaphore()
    for o in range(1, ny):
        pl.semaphore_signal(barrier, inc=1, device_id=to_y(yo(o)), device_id_type=MESH)
    for o in range(1, nz):
        pl.semaphore_signal(barrier, inc=1, device_id=to_z(zo(o)), device_id_type=MESH)
    pl.semaphore_signal(barrier, inc=1, device_id={"dp": partner}, device_id_type=MESH)
    for o in range(1, nx):
        pl.semaphore_signal(
            barrier, inc=1, device_id={"member": lax.rem(mx + o, nx)}, device_id_type=MESH
        )
    pl.semaphore_wait(barrier, ny + nz + nx - 2)

    first, second = pl.ds(0, 64), pl.ds(64, 64)
    order = [half]
    for k in range(half - 1, 0, -1):
        order += [nz - k, k]
    order.append(0)

    for o in range(1, ny):
        send(hs.at[yo(o)], ys_in.at[o - 1], ys_sems, (o - 1,), to_y(yo(o)))
    for o in order:
        send(h.at[over, zo(o), first], t_in.at[0, o], t_sems, (0, o), to_y(up))
        send(h.at[over, zo(o), second], t_in.at[1, o], t_sems, (1, o), to_y(down))
    for o in order:
        landed(t_in.at[0, o], t_sems, (0, o))
        m_out[0, o] = (h[up, zo(o), 0:64].astype(f32) + t_in[0, o].astype(f32)).astype(bf16)
        send(m_out.at[0, o], n_in.at[0, o, first], m_sems, (0, o), to_y(up))
        send(h.at[up, zo(o), second], n_in.at[0, o, second], u_sems, (0, o), to_y(up))
        landed(t_in.at[1, o], t_sems, (1, o))
        m_out[1, o] = (h[down, zo(o), 64:128].astype(f32) + t_in[1, o].astype(f32)).astype(bf16)
        send(m_out.at[1, o], n_in.at[1, o, second], m_sems, (1, o), to_y(down))
        send(h.at[down, zo(o), first], n_in.at[1, o, first], u_sems, (1, o), to_y(down))
    for o in range(1, ny):
        landed(ys_in.at[o - 1], ys_sems, (o - 1,))
    zs_out[...] = hs[y] + sum(ys_in[o - 1] for o in range(1, ny))
    for o in range(1, nz):
        send(zs_out.at[zo(o)], zs_in.at[o - 1], zs_sems, (o - 1,), to_z(zo(o)))

    for o in order:
        landed(n_in.at[0, o, first], m_sems, (0, o))
        landed(n_in.at[0, o, second], u_sems, (0, o))
        landed(n_in.at[1, o, second], m_sems, (1, o))
        landed(n_in.at[1, o, first], u_sems, (1, o))
        value = h[y, zo(o)].astype(f32) + n_in[0, o].astype(f32) + n_in[1, o].astype(f32)
        if o == 0:
            r_out[0] = value
        elif o <= half:
            if o < half:
                landed(r_in.at[o], r_sems, (o,))
                value = value + r_in[o]
            r_out[o] = value
            send(r_out.at[o], r_in.at[o - 1], r_sems, (o - 1,), to_z(zo(1)))
        else:
            if nz - o < half - 1:
                landed(r_in.at[o], r_sems, (o,))
                value = value + r_in[o]
            r_out[o] = value
            send(r_out.at[o], r_in.at[o + 1], r_sems, (o + 1,), to_z(zo(-1)))
    for o in range(1, nz):
        landed(zs_in.at[o - 1], zs_sems, (o - 1,))
    mine_small = zs_out[z] + sum(zs_in[o - 1] for o in range(1, nz))
    landed(r_in.at[0], r_sems, (0,))
    mine = r_out[0] + r_in[0]
    if half > 1:
        landed(r_in.at[nz], r_sems, (nz,))
        mine = mine + r_in[nz]
    block_of(y, z)[...] = mine.T.astype(bf16)

    if half > 1:
        reach = [d for k in range(1, half) for d in (k, -k)]
    else:
        reach = [1]
    for d in reversed(reach):
        ref = block_of(y, z)
        send(ref, ref, gz_sems, (d % nz,), to_z(zo(d)))
    squares = jnp.sum(mine * mine) + jnp.sum(mine_small * mine_small)
    small[c, y, z, :, 0:128] = mine_small
    small[c, y, z, :, 128:256] = jnp.full((1, 128), squares, f32)
    for o in range(1, nz):
        ref = small.at[c, y, z]
        send(ref, ref, gzs_sems, (o - 1,), to_z(zo(o)))

    def along_y(o):
        ref = block_of(y, zo(-o))
        send(ref, ref, gy_sems, (0, o), to_y(up))
        send(ref, ref, gy_sems, (1, o), to_y(down))
        send(ref, ref, pair_sems, (0, o), {"dp": partner})

    def from_y(o):
        zz = zo(-o)
        ref = block_of(down, zz)
        landed(ref, gy_sems, (0, o))
        part = half_of(down, zz, 0)
        send(part, part, go_sems, (0, o), to_y(up))
        send(ref, ref, pair_sems, (1, o), {"dp": partner})
        ref = block_of(up, zz)
        landed(ref, gy_sems, (1, o))
        part = half_of(up, zz, 1)
        send(part, part, go_sems, (1, o), to_y(down))
        send(ref, ref, pair_sems, (2, o), {"dp": partner})

    def from_over(o):
        zz = zo(-o)
        landed(half_of(over, zz, 0), go_sems, (0, o))
        landed(half_of(over, zz, 1), go_sems, (1, o))
        ref = block_of(over, zz)
        send(ref, ref, pair_sems, (3, o), {"dp": partner})

    along_y(0)
    for o in range(1, nz):
        landed(small.at[c, y, zo(-o)], gzs_sems, (o - 1,))
    for o in range(1, ny):
        ref = small.at[c, y]
        send(ref, ref, gys_sems, (o - 1,), to_y(yo(o)))
    items = [0]
    lag = 2
    for d in reach + ([half] if half > 1 else []):
        o = d % nz
        if d == half and half > 1:
            landed(half_of(y, zo(-o), 0), tie_sems, (0,))
            landed(half_of(y, zo(-o), 1), tie_sems, (1,))
        else:
            landed(block_of(y, zo(-o)), gz_sems, (o,))
        if half > 1 and d == half - 1:
            part = half_of(y, zo(-o), 0)
            send(part, part, tie_sems, (0,), to_z(zo(1)))
        if half > 1 and d == 1 - half:
            part = half_of(y, zo(-o), 1)
            send(part, part, tie_sems, (1,), to_z(zo(-1)))
        along_y(o)
        items.append(o)
        if len(items) > lag:
            from_y(items[len(items) - 1 - lag])
    for o in range(1, ny):
        landed(small.at[c, yo(-o)], gys_sems, (o - 1,))
    send(small.at[c], small.at[c], pair_small, (0,), {"dp": partner})
    for o in items[max(0, len(items) - lag) :]:
        from_y(o)
    landed(small.at[1 - c], pair_small, (0,))
    x_out[...] = jnp.sum(small[:, :, :, :, 128:256], axis=(0, 1, 2))
    for o in range(1, nx):
        send(x_out, x_in.at[o - 1], x_sems, (o - 1,), {"member": lax.rem(mx + o, nx)})
    for o in items:
        from_over(o)
    for k in range(2):
        for b in range(ny * nz // 2):
            cut = slice(b * 128, (b + 1) * 128)
            at = b // (nz // 2), 2 * (b % (nz // 2))
            shift_out[k : k + 1, cut] = small[k, at[0], at[1], :, 0:128]
            head_out[k : k + 1, cut] = small[k, at[0], at[1] + 1, :, 0:128]
    for o in range(1, nx):
        landed(x_in.at[o - 1], x_sems, (o - 1,))
    total = x_out[...] + sum(x_in[o - 1] for o in range(1, nx))
    root = math.sqrt(2 * nx * (ny * nz // 2 * 128) * 258)
    factor_out[...] = root / jnp.maximum(jnp.sqrt(total), root)
    for o in items:
        for k in range(4):
            zz = zo(-o)
            yy = (y, down, up, over)[k]
            landed(block_of(yy, zz), pair_sems, (k, o))
    for c in started:
        c.wait_send()


def reduce_all(h, hs, ny, nz, nx):
    f32, bf16 = jnp.float32, jnp.bfloat16
    vmem = pl.BlockSpec(memory_space=pltpu.VMEM)
    dma = pltpu.SemaphoreType.DMA
    hidden = ny * nz // 2 * 128
    return pl.pallas_call(
        functools.partial(reduce_kernel, ny, nz, nx),
        out_shape=(
            jax.ShapeDtypeStruct((2, ny * nz // 2, 128, 256), bf16),
            jax.ShapeDtypeStruct((2, hidden), f32),
            jax.ShapeDtypeStruct((2, hidden), f32),
            jax.ShapeDtypeStruct((1, 128), f32),
        ),
        in_specs=[vmem] * 2,
        out_specs=[vmem] * 4,
        scratch_shapes=[
            pltpu.VMEM((2, nz, 64, 128), bf16),
            pltpu.VMEM((2, nz, 64, 128), bf16),
            pltpu.VMEM((2, nz, 128, 128), bf16),
            pltpu.VMEM((nz, 128, 128), f32),
            pltpu.VMEM((nz + 1, 128, 128), f32),
            pltpu.VMEM((2, ny, nz, 1, 256), f32),
            pltpu.VMEM((ny - 1, nz, 1, 128), f32),
            pltpu.VMEM((nz, 1, 128), f32),
            pltpu.VMEM((nz - 1, 1, 128), f32),
            pltpu.VMEM((1, 128), f32),
            pltpu.VMEM((nx - 1, 1, 128), f32),
            dma((2, 2, nz)),
            dma((2, 2, nz)),
            dma((2, 2, nz)),
            dma((2, nz + 1)),
            dma((2, nz)),
            dma((2, 2)),
            dma((2, 2, nz)),
            dma((2, 2, nz)),
            dma((2, 4, nz)),
            dma((2, ny - 1)),
            dma((2, nz - 1)),
            dma((2, nz - 1)),
            dma((2, ny - 1)),
            dma((2, 1)),
            dma((2, nx - 1)),
        ],
        compiler_params=pltpu.CompilerParams(collective_id=0, has_side_effects=True),
        cost_estimate=pl.CostEstimate(flops=10**7, bytes_accessed=4 * 10**6, transcendentals=0),
        name="gradient_sum",
    )(h, hs)


def dot_nt(a, b):
    return lax.dot_general(a, b, (((1,), (1,)), ((), ())), preferred_element_type=jnp.float32)


def dot_nn(a, b):
    return lax.dot_general(a, b, (((1,), (0,)), ((), ())), preferred_element_type=jnp.float32)


def dot_tn(a, b):
    return lax.dot_general(a, b, (((0,), (0,)), ((), ())), preferred_element_type=jnp.float32)


def iota(shape, axis):
    return lax.broadcasted_iota(jnp.int32, shape, axis)


def ones_where(mask):
    return jnp.where(mask, 1.0, 0.0).astype(jnp.bfloat16)


def dispatch_kernel(
    ny,
    nz,
    nx,
    cap,
    features,
    next_features,
    dest_ref,
    terminal,
    source_ids,
    subset,
    reals,
    target_mean,
    target_scale,
    target_shift,
    target_head,
    w_hbm,
    rows,
    notes,
    target_w1,
    sent,
    sent_notes,
    q_all,
    acc,
    w_sem,
    row_send,
    row_recv,
    note_sems,
    x_sems,
    pair_sems,
    pair_note,
    q_sems,
):
    f32, bf16 = jnp.float32, jnp.bfloat16
    shards = 2 * ny * nz
    flat = 2 * ny
    kept = cap // 2
    tokens, width = features.shape
    me = lax.axis_index("dp")
    mx = lax.axis_index("member")
    c = lax.rem(me, 2)
    z = lax.rem(me // 2, nz)
    y = me // (2 * nz)
    partner = me + 1 - 2 * c
    hh = lax.rem(mx, 2)
    neighbor = mx + 1 - 2 * hh
    fetch = pltpu.make_async_copy(w_hbm, target_w1, w_sem)
    fetch.start()

    def remote(src, dst, send, recv, device):
        return pltpu.make_async_remote_copy(
            src_ref=src, dst_ref=dst, send_sem=send, recv_sem=recv, device_id=device, device_id_type=MESH
        )

    def zo(o):
        return lax.rem(z + nz + o, nz)

    def group(oz, skip, act):
        for j in range(flat):
            oy, oc = j // 2, j % 2
            if skip and j == 0:
                continue
            yy = lax.rem(y + oy, ny)
            cc = lax.rem(c + oc, 2)
            zz = zo(oz)
            act(oz, (yy * nz + zz) * 2 + cc, zz * flat + yy * 2 + cc, cc)

    def each(act):
        def step(i, _):
            group(far_first(i, nz), False, act)
            return 0

        lax.fori_loop(0, nz - 1, step, 0)
        group(0, True, act)

    barrier = pltpu.get_barrier_semaphore()

    def greet(oz, to, place, cc):
        pl.semaphore_signal(barrier, inc=1, device_id={"dp": to}, device_id_type=MESH)

    each(greet)
    for o in range(1, nx):
        pl.semaphore_signal(
            barrier, inc=1, device_id={"member": lax.rem(mx + o, nx)}, device_id_type=MESH
        )

    dest = dest_ref[...]
    dest = ((dest >> 1) & (nz - 1)) * flat + (dest // (2 * nz)) * 2 + (dest & 1)
    to_shard = dest == iota((shards, tokens), 0)
    chosen = ones_where(to_shard)
    before = ones_where(iota((tokens, tokens), 0) < iota((tokens, tokens), 1))
    rank = jnp.sum(jnp.where(to_shard, dot_nn(chosen, before), 0.0), axis=0, keepdims=True)
    rank = rank.astype(jnp.int32)
    low = rank - hh * kept
    slot = jnp.where((low >= 0) & (low < kept), dest * kept + low, -1)
    chunk = min(256, shards * kept)
    per = chunk // kept
    for i in range(shards // per):
        pick = ones_where(iota((chunk, tokens), 0) + i * chunk == slot)
        block = dot_nn(pick, features[...]).astype(bf16)
        sent[i * per : (i + 1) * per] = block.reshape(per, kept, width)

    pl.semaphore_wait(barrier, shards + nx - 2)

    def send_rows(oz, to, place, cc):
        remote(
            sent.at[place],
            rows.at[cc, hh, z, y * 2 + c],
            row_send,
            row_recv.at[lax.rem(oz, nz)],
            {"dp": to},
        ).start()

    each(send_rows)
    rows[c, hh, z, y * 2 + c] = sent[z * flat + y * 2 + c]

    weight = jnp.zeros((1, tokens), f32)
    for k in range(reals.shape[1] - 2 * tokens - 120):
        value = reals[:, 2 * tokens + k : 2 * tokens + k + 1]
        weight = jnp.where(source_ids[...] == k, value, weight)

    hidden = target_w1.shape[1]
    wide = min(256, hidden)
    tall = min(128, tokens)
    acc[...] = jnp.zeros(acc.shape, f32)
    fetch.wait()
    for k in range(2):

        def block(i, _, k=k):
            units = pl.ds(pl.multiple_of(i * wide, wide), wide)
            scale = target_scale[k : k + 1, units]
            shift = target_shift[k : k + 1, units] - target_mean[k : k + 1, units] * scale
            head = target_head[k : k + 1, units]
            w = target_w1[k, units, :]
            for t in range(tokens // tall):
                pre = dot_nt(next_features[t * tall : (t + 1) * tall, :], w)
                term = jnp.maximum(pre * scale + shift, 0.0) * head
                total = term[:, 0:128]
                for part in range(1, wide // 128):
                    total = total + term[:, part * 128 : (part + 1) * 128]
                acc[k, t * tall : (t + 1) * tall, :] += total
            return 0

        lax.fori_loop(0, hidden // wide, block, 0)
        q_all[mx, k] = jnp.sum(acc[k].T, axis=0, keepdims=True)

    def q_copy(o):
        ref = q_all.at[mx]
        return remote(ref, ref, q_sems.at[0, o - 1], q_sems.at[1, o - 1], {"member": lax.rem(mx + o, nx)})

    for o in range(1, nx):
        q_copy(o).start()

    half = nz // 2
    arrivals = [0] + [o % nz for k in range(1, half) for o in (k, -k)] + [half]

    def x_copy(o):
        ref = rows.at[c, hh, zo(-o)]
        return remote(ref, ref, x_sems.at[0, o], x_sems.at[1, o], {"member": neighbor})

    def pair_copy(part, o):
        ref = rows.at[c, hh + part - 2 * hh * part, zo(-o)]
        return remote(ref, ref, pair_sems.at[0, part, o], pair_sems.at[1, part, o], {"dp": partner})

    def arrive(o):
        ref = rows.at[c, hh, zo(-o)]
        if o == 0:
            ref = rows.at[c, hh, z, pl.ds(0, flat - 1)]
        remote(ref, ref, row_send, row_recv.at[o], {"dp": partner}).wait_recv()
        x_copy(o).start()
        pair_copy(0, o).start()

    early = nz // 2
    for o in arrivals[:early]:
        arrive(o)

    for o in range(1, nx):
        q_copy(o).wait_recv()
    first = jnp.zeros((1, tokens), f32)
    second = first
    for k in range(2 * nx):
        value = q_all[k // 2, k % 2]
        first = jnp.where(subset[0:1, :] == k, value, first)
        second = jnp.where(subset[1:2, :] == k, value, second)
    lowest = jnp.minimum(first, second)
    carry = 1.0 - terminal[...].astype(f32)
    target = reals[:, 0:tokens] + GAMMA * carry * (lowest - ALPHA * reals[:, tokens : 2 * tokens])

    lane = iota((128, tokens), 0)
    spread = jnp.where(to_shard, target, 0.0).astype(bf16)
    spread_w = jnp.where(to_shard, weight, 0.0).astype(bf16)
    note = dot_nt(spread, ones_where(lane == rank)) + dot_nt(spread_w, ones_where(lane == rank + cap))
    sent_notes[...] = note.reshape(shards, 1, 128)
    mine = z * flat + y * 2 + c

    def send_notes(oz, to, place, cc):
        remote(
            sent_notes.at[place], notes.at[cc, mine], note_sems.at[0], note_sems.at[1], {"dp": to}
        ).start()

    each(send_notes)
    notes[c, mine] = sent_notes[mine]

    for o in arrivals[early:]:
        arrive(o)
    for o in arrivals:
        x_copy(o).wait_recv()
        pair_copy(1, o).start()
    most = notes.at[c, pl.ds(0, shards - 1)]
    all_notes = remote(most, most, note_sems.at[0], note_sems.at[1], {"dp": partner})
    all_notes.wait_recv()
    pair_n = remote(notes.at[c], notes.at[c], pair_note.at[0], pair_note.at[1], {"dp": partner})
    pair_n.start()

    all_notes.wait_send()
    most = sent.at[pl.ds(0, shards - 1)]
    remote(most, most, row_send, row_recv.at[0], {"dp": partner}).wait_send()
    for o in range(1, nx):
        q_copy(o).wait_send()
    for o in arrivals:
        x_copy(o).wait_send()
        pair_copy(0, o).wait()
        pair_copy(1, o).wait()
    pair_n.wait()


def dispatch(features, next_features, dest, terminal, source_ids, subset, reals, targets, ny, nz, nx):
    tokens, width = features.shape
    shards = 2 * ny * nz
    cap = 2 * tokens // shards
    f32, bf16 = jnp.float32, jnp.bfloat16
    vmem = pl.BlockSpec(memory_space=pltpu.VMEM)
    dma = pltpu.SemaphoreType.DMA
    w1 = targets[0]
    return pl.pallas_call(
        functools.partial(dispatch_kernel, ny, nz, nx, cap),
        out_shape=(
            jax.ShapeDtypeStruct((2, 2, nz, 2 * ny, cap // 2, width), bf16),
            jax.ShapeDtypeStruct((2, shards, 1, 128), f32),
        ),
        in_specs=[vmem] * 11 + [pl.BlockSpec(memory_space=pl.ANY)],
        out_specs=[vmem] * 2,
        scratch_shapes=[
            pltpu.VMEM(w1.shape, w1.dtype),
            pltpu.VMEM((shards, cap // 2, width), bf16),
            pltpu.VMEM((shards, 1, 128), f32),
            pltpu.VMEM((nx, 2, 1, tokens), f32),
            pltpu.VMEM((2, tokens, 128), f32),
            dma,
            dma,
            dma((nz,)),
            dma((2,)),
            dma((2, nz)),
            dma((2, 2, nz)),
            dma((2,)),
            dma((2, nx - 1)),
        ],
        compiler_params=pltpu.CompilerParams(collective_id=1, has_side_effects=True),
        cost_estimate=pl.CostEstimate(flops=10**9, bytes_accessed=4 * 10**6, transcendentals=0),
        name="dispatch",
    )(features, next_features, dest, terminal, source_ids, subset, reals, *targets[1:], w1)


def critic_kernel(
    cap,
    tile,
    rows,
    notes,
    shift_all,
    head_all,
    w_hbm,
    h,
    hs,
    w_wide,
    w,
    xc,
    targets,
    weights,
    zbuf,
    gbuf,
    gz,
    gt,
    sq,
    s0,
    s1,
    sem,
):
    f32, bf16 = jnp.float32, jnp.bfloat16
    slots, width = rows.shape[1:]
    hidden = w.shape[0]
    shards = slots // cap
    pieces = slots // 128
    few, many = 3, 6
    wide = min(256, hidden)
    lanes = hidden // 128
    c = lax.rem(lax.axis_index("dp"), 2)
    fetch = pltpu.make_async_copy(w_hbm.at[c], w_wide, sem)
    fetch.start()
    shift = shift_all[pl.ds(c, 1), :]
    head = head_all[pl.ds(c, 1), :]

    kept, part = cap // 2, slots // 2
    at_slot = iota((1, slots), 1)
    owner = ones_where(lax.rem(at_slot, part) // kept == iota((shards, slots), 0))
    my_slot = at_slot // part * kept + lax.rem(at_slot, kept) == iota((cap, slots), 0)
    upto = ones_where(iota((128, 128), 0) <= iota((128, 128), 1))
    counts = []
    for s in range(2):
        by_slot = notes[s, :, 0, :].T[0 : 2 * cap].astype(bf16)
        spread = dot_nn(by_slot, owner)
        y_row = jnp.sum(jnp.where(my_slot, spread[0:cap], 0.0), axis=0, keepdims=True)
        w_row = jnp.sum(jnp.where(my_slot, spread[cap : 2 * cap], 0.0), axis=0, keepdims=True)
        alive = jnp.where(w_row > 0, 1.0, 0.0)
        stacked = jnp.concatenate(
            [alive[:, p * 128 : (p + 1) * 128] for p in range(pieces)]
            + [jnp.zeros((8, 128), f32)] * (1 if pieces < 8 else 0),
            axis=0,
        )
        running = dot_nn(stacked.astype(bf16), upto)
        place = []
        start = jnp.zeros((1, 1), f32)
        for p in range(pieces):
            position = running[p : p + 1] - 1.0 + start
            position = jnp.where(stacked[p : p + 1] > 0, position, -1.0)
            place.append(position.astype(jnp.int32))
            start = start + running[p : p + 1, 127:128]
        number = jnp.sum(alive)
        counts.append(number)
        y_wide = jnp.broadcast_to(y_row, (128, slots)).astype(bf16)
        w_wide_row = jnp.broadcast_to(w_row, (128, slots)).astype(bf16)
        trips = jnp.where(number <= few * tile, few, many)

        def compact(i, _, s=s, place=place, y_wide=y_wide, w_wide_row=w_wide_row):
            at = pl.ds(pl.multiple_of(i * tile, tile), tile)
            row = iota((tile, 128), 0) + i * tile
            pick = jnp.concatenate([ones_where(row == p) for p in place], axis=1)
            xc[s, at, :] = dot_nn(pick, rows[s]).astype(bf16)
            targets[s, at, :] = dot_nt(pick, y_wide)
            weights[s, at, :] = dot_nt(pick, w_wide_row)
            return 0

        lax.fori_loop(0, trips, compact, 0)

    fetch.wait()
    w[...] = w_wide[...].astype(bf16)
    total0 = jnp.zeros((1, hidden), f32)
    total1 = jnp.zeros((1, hidden), f32)
    groups = tile // 8
    for s in range(2):
        number = counts[s]
        whole = jnp.full((1, 1), number, f32)
        trips = jnp.where(number <= few * tile, few, many)
        middle = jnp.sum(rows[s].astype(f32), axis=0, keepdims=True) / whole
        one = middle.astype(bf16)
        rest = middle - one.astype(f32)
        two = rest.astype(bf16)
        three = (rest - two.astype(f32)).astype(bf16)
        parts = jnp.concatenate(
            [one.astype(f32), two.astype(f32), three.astype(f32), jnp.zeros((13, width), f32)], axis=0
        ).astype(bf16)
        mu = jnp.sum(dot_nt(parts, w[...]), axis=0, keepdims=True)
        sq[...] = jnp.zeros(sq.shape, f32)
        s0[...] = jnp.zeros(s0.shape, f32)
        s1[...] = jnp.zeros(s1.shape, f32)

        def forward(i, _, s=s, mu=mu, number=number):
            at = pl.ds(pl.multiple_of(i * tile, tile), tile)
            row = iota((tile, 128), 0) + i * tile
            alive = jnp.where(row < number.astype(jnp.int32), 1.0, 0.0)
            x = xc[s, at, :]
            for j in range(hidden // wide):
                pre = dot_nt(x, w[j * wide : (j + 1) * wide, :])
                for k in range(wide // 128):
                    lo = j * wide + k * 128
                    zc = (pre[:, k * 128 : (k + 1) * 128] - mu[:, lo : lo + 128]) * alive
                    zbuf[at, lo : lo + 128] = zc
                    sq[:, lo : lo + 128] += jnp.sum((zc * zc).reshape(groups, 8, 128), axis=0)
            return 0

        lax.fori_loop(0, trips, forward, 0)
        var = jnp.sum(sq[...], axis=0, keepdims=True) / whole
        inv = 1.0 / jnp.sqrt(var + EPS)

        def slopes(i, _, s=s, inv=inv):
            at = pl.ds(pl.multiple_of(i * tile, tile), tile)
            acc = jnp.zeros((tile, 128), f32)
            for j in range(lanes):
                cut = slice(j * 128, (j + 1) * 128)
                zh = zbuf[at, cut] * inv[:, cut]
                zbuf[at, cut] = zh
                acc = acc + jnp.maximum(zh + shift[:, cut], 0.0) * head[:, cut]
            q = jnp.sum(acc, axis=1, keepdims=True)
            dq = weights[s, at, :] * (q - targets[s, at, :])
            for j in range(lanes):
                cut = slice(j * 128, (j + 1) * 128)
                zh = zbuf[at, cut]
                g = jnp.where(zh > -shift[:, cut], dq, 0.0)
                gbuf[at, cut] = g
                s0[:, cut] += jnp.sum(g.reshape(groups, 8, 128), axis=0)
                s1[:, cut] += jnp.sum((g * zh).reshape(groups, 8, 128), axis=0)
            return 0

        lax.fori_loop(0, trips, slopes, 0)
        sum0 = jnp.sum(s0[...], axis=0, keepdims=True)
        sum1 = jnp.sum(s1[...], axis=0, keepdims=True)
        total0 = total0 + sum0
        total1 = total1 + sum1
        scale = inv * head
        base = -scale * (sum0 / whole)
        tilt = -scale * (sum1 / whole)

        def backward(i, _, scale=scale, base=base, tilt=tilt):
            at = pl.ds(pl.multiple_of(i * tile, tile), tile)
            for j in range(lanes):
                cut = slice(j * 128, (j + 1) * 128)
                value = gbuf[at, cut] * scale[:, cut] + (zbuf[at, cut] * tilt[:, cut] + base[:, cut])
                gz[at, cut] = value.astype(bf16)
            return 0

        lax.fori_loop(0, trips, backward, 0)

        def product(depth, s=s):
            x = xc[s, 0:depth, :]
            for j in range(hidden // wide):
                cut = slice(j * wide, (j + 1) * wide)
                out = dot_tn(x, gz[0:depth, cut])
                gt[:, cut] = out if s == 0 else gt[:, cut] + out

        @pl.when(trips == few)
        def _():
            product(few * tile)

        @pl.when(trips != few)
        def _():
            product(many * tile)

    g_shift = head * total0
    g_head = shift * total0 + total1
    for u in range(lanes):
        cut = slice(u * 128, (u + 1) * 128)
        h[2 * u] = gt[0:128, cut].astype(bf16)
        h[2 * u + 1] = gt[128:256, cut].astype(bf16)
        hs[2 * u] = g_shift[:, cut]
        hs[2 * u + 1] = g_head[:, cut]


def critic_sums(rows, notes, shift, head, w1, cap):
    f32, bf16 = jnp.float32, jnp.bfloat16
    slots, width = rows.shape[1:]
    hidden = w1.shape[1]
    tile = slots * 3 // 16
    tall = 6 * tile
    vmem = pl.BlockSpec(memory_space=pltpu.VMEM)
    blocks = hidden // 128 * (width // 128)
    return pl.pallas_call(
        functools.partial(critic_kernel, cap, tile),
        out_shape=(
            jax.ShapeDtypeStruct((blocks, 128, 128), bf16),
            jax.ShapeDtypeStruct((blocks, 1, 128), f32),
        ),
        in_specs=[vmem] * 4 + [pl.BlockSpec(memory_space=pl.ANY)],
        out_specs=[vmem] * 2,
        scratch_shapes=[
            pltpu.VMEM((hidden, width), f32),
            pltpu.VMEM((hidden, width), bf16),
            pltpu.VMEM((2, tall, width), bf16),
            pltpu.VMEM((2, tall, 128), f32),
            pltpu.VMEM((2, tall, 128), f32),
            pltpu.VMEM((tall, hidden), f32),
            pltpu.VMEM((tall, hidden), f32),
            pltpu.VMEM((tall, hidden), bf16),
            pltpu.VMEM((width, hidden), f32),
            pltpu.VMEM((8, hidden), f32),
            pltpu.VMEM((8, hidden), f32),
            pltpu.VMEM((8, hidden), f32),
            pltpu.SemaphoreType.DMA,
        ],
        compiler_params=pltpu.CompilerParams(vmem_limit_bytes=60 * 2**20),
        cost_estimate=pl.CostEstimate(
            flops=8 * slots * hidden * width, bytes_accessed=4 * 10**6, transcendentals=0
        ),
        name="critic_sums",
    )(rows, notes, shift, head, w1)


def per_device(
    features,
    next_features,
    rewards,
    next_logp,
    terminal,
    source_ids,
    source_weight,
    subset,
    destination,
    critic_w1,
    critic_shift,
    critic_head,
    target_w1,
    target_mean,
    target_scale,
    target_shift,
    target_head,
):
    f32 = jnp.float32
    shards = lax.axis_size("dp")
    nx = lax.axis_size("member")
    nz = NZ
    ny = shards // (2 * nz)
    tokens, width = features.shape
    critics, hidden = critic_w1.shape[:2]
    cap = 2 * tokens // shards
    reals = jnp.concatenate(
        [
            rewards.astype(f32),
            next_logp.astype(f32),
            source_weight.astype(f32),
            jnp.zeros((120,), f32),
        ]
    )
    rows, notes = dispatch(
        features,
        next_features,
        destination.reshape(1, tokens),
        terminal.reshape(1, tokens),
        source_ids.reshape(1, tokens),
        subset.T,
        reals.reshape(1, 2 * tokens + 128),
        (target_w1, target_mean, target_scale, target_shift, target_head),
        ny,
        nz,
        nx,
    )
    h, hs = critic_sums(
        rows.reshape(2, shards * cap, width), notes, critic_shift, critic_head, critic_w1, cap
    )
    h = h.reshape(ny, nz, 128, 128)
    hs = hs.reshape(ny, nz, 1, 128)
    full, shift, head, factor = reduce_all(h, hs, ny, nz, nx)
    factor = factor[0, 0]
    step_w1 = full.reshape(critics, hidden, width).astype(f32) * factor
    return (step_w1, shift * factor, head * factor)


def solution(mesh):
    in_specs = (
        P("dp", None),
        P("dp", None),
        P("dp"),
        P("dp"),
        P("dp"),
        P("dp"),
        P(),
        P("dp", None),
        P("dp"),
        P("member", None, None),
        P("member", None),
        P("member", None),
        P("member", None, None),
        P("member", None),
        P("member", None),
        P("member", None),
        P("member", None),
    )
    out_specs = (P("member", None, None), P("member", None), P("member", None))
    return jax.shard_map(
        per_device, mesh=mesh, in_specs=in_specs, out_specs=out_specs, check_vma=False
    )
```

time: 117 us -> 113 us (0.966)
  local copies, waits for them, and re-layouts: 4.86 us -> 2.72 us
  Pallas kernels: 105 us -> 103 us
    pallas_call x1, Pallas kernels: 38 us -> 30 us  [dispatch(): pl.pallas_call(functools.partial(dispatch_kernel, ny, nz, nx, cap), out_s...]
    pallas_call x1, Pallas kernels: 47.6 us -> 53.8 us  [reduce_all(): pl.pallas_call(functools.partial(reduce_kernel, ny, nz, nx), out_shape=(j...]
    another operation x6 -> x0, local copies, waits for them, and re-layouts: 3.48 us -> none  [the longest x4 2.11 us: per_device(): jnp.stack([terminal, source_ids, subset[:, 0], subset[:, 1], destination,...]
    concatenate x0 -> x1, local copies, waits for them, and re-layouts: none -> 2.12 us  [per_device(): jnp.concatenate([rewards.astype(f32), next_logp.astype(f32), source_weigh...]
    mul x1, other arithmetic: 0.09 us -> 1.92 us  [per_device(): return (step_w1, shift * factor, head * factor)]
    convert_element_type x2 -> x0, other arithmetic: 1.77 us -> none  [the longest x1 1.17 us: per_device(): source_weight.astype(f32)]
where the time goes in v3:
time: 113 us
  Pallas kernels  103 us (91%)
  other arithmetic  6.61 us (6%)
  local copies, waits for them, and re-layouts  2.72 us (2%)
    pallas_call x1, Pallas kernels, reduce_all(): pl.pallas_call(functools.partial(reduce_kernel, ny, nz, nx), out_shape=(j...  53.8 us
    pallas_call x1, Pallas kernels, dispatch(): pl.pallas_call(functools.partial(dispatch_kernel, ny, nz, nx, cap), out_s...  30 us
    pallas_call x1, Pallas kernels, critic_sums(): pl.pallas_call(functools.partial(critic_kernel, cap, tile), out_shape=(ja...  19.1 us
    mul x1, other arithmetic, per_device(): step_w1 = full.reshape(critics, hidden, width).astype(f32) * factor  4.69 us

profile of v3, /device:TPU:1, one launch (start us, length us, event | category | flops | bytes accessed | tf_op | source)
XLA Modules:
  0.0 112.9 jit_solution(9142055466432741987)
XLA Ops:
  0.6 2.1 %concatenate.3 = f32[1152]{0:T(1024)S(1)} concatenate(bf16[512]{0:T(512)(128)(2,1)} %param.19, bf16[512]{0:T(512)(128)(2,1)} %param.20, bf16[8]{0:T(256)(128)(2,1)} %param.23, f32[120]{0:T(128)S(1)} %broadcast_in_dim.3), dimensions={0} | concatenate | bytes 7152 | tf_op jit(solution)/shard_map/concatenate | solution.py:863
  2.8 0.6 reshape.34.reals
  3.4 30.0 %dispatch.1 = (bf16[2,2,8,8,8,256]{5,4,3,2,1,0:T(8,128)(2,1)}, f32[2,64,1,128]{3,2,1,0:T(1,128)}) custom-call(bf16[512,256]{1,0:T(8,128)(2,1)} %features.1, bf16[512,256]{1,0:T(8,128)(2,1)} %next_features.1, s32[1,512]{1,0:T(1,128)} %bitcast.16, s32[1,512]{1,0:T(1,128)} %bitcast.17, s32[1,512]{1,0:T(1,128)} %bitcast.18, s32[2,512]{1,0:T(2,128)} %bitcast.15, ...), custom_call_target="tpu_custom_call" | custom-call | flops 1000000000 | bytes 4000000 | tf_op jit(solution)/shard_map/dispatch/pallas_call | solution.py:585
  33.4 19.1 %critic_sums.1 = (bf16[32,128,128]{2,1,0:T(8,128)(2,1)}, f32[32,1,128]{2,1,0:T(1,128)}) custom-call(bf16[2,1024,256]{2,1,0:T(8,128)(2,1)} %bitcast.19, f32[2,64,1,128]{3,2,1,0:T(1,128)} %get-tuple-element.12.notes, f32[2,2048]{1,0:T(2,128)} %shift_all.1, f32[2,2048]{1,0:T(2,128)} %head_all.1, f32[2,2048,256]{2,1,0:T(8,128)} %w_hbm.3), custom_call_target="tpu_custom_call" | custom-call | flops 4294967296 | bytes 4000000 | tf_op jit(solution)/shard_map/critic_sums/pallas_call | solution.py:805
  52.5 53.8 %gradient_sum.1 = (bf16[2,16,128,256]{3,2,1,0:T(8,128)(2,1)}, f32[2,2048]{1,0:T(2,128)}, f32[2,2048]{1,0:T(2,128)}, f32[1,128]{1,0:T(1,128)}) custom-call(bf16[4,8,128,128]{3,2,1,0:T(8,128)(2,1)} %bitcast.11, f32[4,8,1,128]{3,2,1,0:T(1,128)} %bitcast.12), custom_call_target="tpu_custom_call" | custom-call | flops 10000000 | bytes 4000000 | tf_op jit(solution)/shard_map/gradient_sum/pallas_call | solution.py:287
  106.2 1.9 %broadcast_multiply_fusion = (f32[2,2048]{1,0:T(2,128)}, f32[2,2048]{1,0:T(2,128)}) fusion(f32[2,2048]{1,0:T(2,128)} %get-tuple-element.18, f32[]{:T(128)} %bitcast.13, f32[2,2048]{1,0:T(2,128)} %get-tuple-element.17), kind=kLoop, calls=%fused_computation.1 | loop fusion | flops 8192 | bytes 65540 | tf_op jit(solution)/shard_map/mul | solution.py:892
  108.2 4.7 %convert_multiply_fusion = f32[2,16,128,256]{3,2,1,0:T(8,128)} fusion(bf16[2,16,128,256]{3,2,1,0:T(8,128)(2,1)} %get-tuple-element.15, f32[]{:T(128)} %bitcast.14), kind=kLoop, calls=%fused_computation | loop fusion | flops 2097152 | bytes 6291460 | tf_op jit(solution)/shard_map/mul | solution.py:891
  (1 shorter events, 0.0 us)

commit v4 on v2

--- a/solution.py
+++ b/solution.py
@@ -31,8 +31,10 @@
     h,
     hs,
     full,
+    shift_out,
+    head_out,
+    factor_out,
     small,
-    total,
     y_in,
     z_out,
     z_in,
@@ -80,7 +82,9 @@
         )
 
     def block_of(yy, zz):
-        return full.at[c, yy * (nz // 2) + zz // 2, :, pl.ds(pl.multiple_of(lax.rem(zz, 2) * 128, 128), 128)]
+        return full.at[
+            c, yy * (nz // 2) + zz // 2, :, pl.ds(pl.multiple_of(lax.rem(zz, 2) * 128, 128), 128)
+        ]
 
     barrier = pltpu.get_barrier_semaphore()
     for o in range(1, ny):
@@ -162,8 +166,7 @@
     squares = jnp.sum(mine * mine) + jnp.sum(mine_small * mine_small)
     small[c, y, z, :, 0:128] = mine_small
     small[c, y, z, :, 128:256] = jnp.full((1, 128), squares, jnp.float32)
-    mine_ref = block_of(y, z)
-    mine_ref[...] = mine.T.astype(jnp.bfloat16)
+    block_of(y, z)[...] = mine.T.astype(jnp.bfloat16)
 
     def gz_small(o):
         ref = small.at[c, y, z]
@@ -189,7 +192,7 @@
         gz_small(o).start()
 
     def send_gz(i, _):
-        gz_block(far_first(i, nz)).start()
+        gz_block(near_first(i, nz)).start()
         return 0
 
     lax.fori_loop(0, nz - 1, send_gz, 0)
@@ -244,7 +247,15 @@
     lax.fori_loop(half, nz, relay_y, 0)
     for o in range(1, nx):
         x_copy(o).wait_recv()
-    total[...] = x_out[...] + sum(x_in[o - 1] for o in range(1, nx))
+    total = x_out[...] + sum(x_in[o - 1] for o in range(1, nx))
+    root = math.sqrt(2 * nx * (ny * nz // 2 * 128) * 258)
+    factor_out[...] = root / jnp.maximum(jnp.sqrt(total), root)
+    for k in range(2):
+        for b in range(ny * nz // 2):
+            cut = slice(b * 128, (b + 1) * 128)
+            at = b // (nz // 2), 2 * (b % (nz // 2))
+            shift_out[k : k + 1, cut] = small[k, at[0], at[1], :, 0:128]
+            head_out[k : k + 1, cut] = small[k, at[0], at[1] + 1, :, 0:128]
 
     def wait_pair(i, _):
         for o in range(ny):
@@ -288,13 +299,15 @@
     return pl.pallas_call(
         functools.partial(reduce_kernel, ny, nz, nx),
         out_shape=(
-            jax.ShapeDtypeStruct((2, ny * nz // 2, 128, 256), bf16),
-            jax.ShapeDtypeStruct((2, ny, nz, 1, 256), f32),
-            jax.ShapeDtypeStruct((1, 128), f32),
+            pltpu.VMEM((2, ny * nz // 2, 128, 256), bf16),
+            pltpu.VMEM((2, ny * nz // 2 * 128), f32),
+            pltpu.VMEM((2, ny * nz // 2 * 128), f32),
+            pltpu.VMEM((1, 128), f32),
         ),
         in_specs=[vmem] * 2,
-        out_specs=[vmem] * 3,
+        out_specs=[vmem] * 4,
         scratch_shapes=[
+            pltpu.VMEM((2, ny, nz, 1, 256), f32),
             pltpu.VMEM((ny - 1, nz, rows, width), bf16),
             pltpu.VMEM((nz, rows, width), f32),
             pltpu.VMEM((nz, rows, width), f32),
@@ -315,7 +328,9 @@
             dma((2, 1)),
             dma((2, nx - 1)),
         ],
-        compiler_params=pltpu.CompilerParams(collective_id=0, has_side_effects=True),
+        compiler_params=pltpu.CompilerParams(
+            collective_id=0, has_side_effects=True, vmem_limit_bytes=44 * 2**20
+        ),
         cost_estimate=pl.CostEstimate(flops=10**7, bytes_accessed=4 * 10**6, transcendentals=0),
         name="gradient_sum",
     )(h, hs)
@@ -348,112 +363,141 @@
     cap,
     features,
     next_features,
-    ints,
-    reals,
+    dest_ref,
+    terminal,
+    source_ids,
+    subset,
+    rewards,
+    next_logp,
     source_weight,
-    target_w1,
+    critic_shift,
+    critic_head,
     target_mean,
     target_scale,
     target_shift,
     target_head,
+    w_hbm,
+    critic_hbm,
     rows,
     notes,
+    shift_out,
+    head_out,
+    critic_out,
+    target_w1,
+    critic_w1,
     sent,
     sent_notes,
     q_all,
     acc,
-    row_sems,
+    w_sem,
+    critic_sem,
+    row_send,
+    row_recv,
     note_sems,
+    x_sems,
     pair_sems,
     pair_note,
     q_sems,
 ):
     f32, bf16 = jnp.float32, jnp.bfloat16
     shards = 2 * ny * nz
-    tokens = features.shape[0]
+    flat = 2 * ny
+    kept = cap // 2
+    tokens, width = features.shape
     me = lax.axis_index("dp")
     mx = lax.axis_index("member")
     c = lax.rem(me, 2)
     z = lax.rem(me // 2, nz)
     y = me // (2 * nz)
     partner = me + 1 - 2 * c
-
-    def peer(i, sign):
-        oc = lax.rem(i, 2)
-        oz = lax.rem(far_first(lax.rem(i // 2, nz), nz), nz)
-        oy = i // (2 * nz)
-        yy = lax.rem(y + ny + sign * oy, ny)
-        zz = lax.rem(z + nz + sign * oz, nz)
-        return (yy * nz + zz) * 2 + lax.rem(c + oc, 2)
-
-    last = 2 * nz - 2
-
-    def step_of(i):
-        return i + jnp.where(i >= last, 1, 0)
+    hh = lax.rem(mx, 2)
+    neighbor = mx + 1 - 2 * hh
+    fetch = pltpu.make_async_copy(w_hbm, target_w1, w_sem)
+    fetch.start()
+    fetch_critic = pltpu.make_async_copy(critic_hbm.at[c], critic_w1, critic_sem)
+    fetch_critic.start()
+
+    def as_row(ref):
+        wide = ref[...].astype(f32)
+        return jnp.concatenate([wide[i : i + 1] for i in range(wide.shape[0])], axis=1)
 
     def remote(src, dst, send, recv, device):
         return pltpu.make_async_remote_copy(
             src_ref=src, dst_ref=dst, send_sem=send, recv_sem=recv, device_id=device, device_id_type=MESH
         )
 
+    def zo(o):
+        return lax.rem(z + nz + o, nz)
+
+    def group(oz, skip, act):
+        for j in range(flat):
+            oy, oc = j // 2, j % 2
+            if skip and j == 0:
+                continue
+            yy = lax.rem(y + oy, ny)
+            cc = lax.rem(c + oc, 2)
+            zz = zo(oz)
+            act(oz, (yy * nz + zz) * 2 + cc, zz * flat + yy * 2 + cc, cc)
+
+    def each(act):
+        def step(i, _):
+            group(far_first(i, nz), False, act)
+            return 0
+
+        lax.fori_loop(0, nz - 1, step, 0)
+        group(0, True, act)
+
     barrier = pltpu.get_barrier_semaphore()
 
-    def greet(i, _):
-        pl.semaphore_signal(
-            barrier, inc=1, device_id={"dp": peer(step_of(i), 1)}, device_id_type=MESH
-        )
-        return 0
-
-    lax.fori_loop(0, shards - 1, greet, 0)
+    def greet(oz, to, place, cc):
+        pl.semaphore_signal(barrier, inc=1, device_id={"dp": to}, device_id_type=MESH)
+
+    each(greet)
     for o in range(1, nx):
         pl.semaphore_signal(
             barrier, inc=1, device_id={"member": lax.rem(mx + o, nx)}, device_id_type=MESH
         )
 
-    dest = ints[4:5, :]
+    dest = dest_ref[...]
+    dest = ((dest >> 1) & (nz - 1)) * flat + (dest // (2 * nz)) * 2 + (dest & 1)
     to_shard = dest == iota((shards, tokens), 0)
     chosen = ones_where(to_shard)
     before = ones_where(iota((tokens, tokens), 0) < iota((tokens, tokens), 1))
     rank = jnp.sum(jnp.where(to_shard, dot_nn(chosen, before), 0.0), axis=0, keepdims=True)
     rank = rank.astype(jnp.int32)
-    slot = dest * cap + rank
-    chunk = min(16, shards) * cap
-    per = min(16, shards)
-
-    def place(i, _):
+    low = rank - hh * kept
+    slot = jnp.where((low >= 0) & (low < kept), dest * kept + low, -1)
+    chunk = min(256, shards * kept)
+    per = chunk // kept
+    for i in range(shards // per):
         pick = ones_where(iota((chunk, tokens), 0) + i * chunk == slot)
         block = dot_nn(pick, features[...]).astype(bf16)
-        sent[pl.ds(i * per, per)] = block.reshape(per, cap, features.shape[1])
-        return 0
-
-    lax.fori_loop(0, shards // per, place, 0)
+        sent[i * per : (i + 1) * per] = block.reshape(per, kept, width)
+
+    pl.semaphore_wait(barrier, shards + nx - 2)
+
+    def send_rows(oz, to, place, cc):
+        remote(
+            sent.at[place],
+            rows.at[cc, hh, z, y * 2 + c],
+            row_send,
+            row_recv.at[lax.rem(oz, nz)],
+            {"dp": to},
+        ).start()
+
+    each(send_rows)
+    rows[c, hh, z, y * 2 + c] = sent[z * flat + y * 2 + c]
+
     weight = jnp.zeros((1, tokens), f32)
-    for k in range(source_weight.shape[0]):
-        weight = jnp.where(ints[1:2, :] == k, source_weight[k], weight)
-
-    pl.semaphore_wait(barrier, shards + nx - 2)
-
-    def row_copy(i):
-        to = peer(i, 1)
-        return remote(
-            sent.at[to], rows.at[lax.rem(to, 2), me], row_sems.at[0, i], row_sems.at[1, i], {"dp": to}
-        )
-
-    def row_landed(i):
-        ref = rows.at[c, peer(i, -1)]
-        return remote(ref, ref, row_sems.at[0, i], row_sems.at[1, i], {"dp": peer(i, 1)})
-
-    def send_rows(i, _):
-        row_copy(step_of(i)).start()
-        return 0
-
-    lax.fori_loop(0, shards - 1, send_rows, 0)
-    rows[c, me] = sent[me]
+    weights = source_weight[...].astype(f32)
+    for k in range(weights.shape[1]):
+        weight = jnp.where(source_ids[...] == k, weights[:, k : k + 1], weight)
 
     hidden = target_w1.shape[1]
     wide = min(256, hidden)
-    tall = 128 if tokens % 128 == 0 else tokens
+    tall = min(128, tokens)
     acc[...] = jnp.zeros(acc.shape, f32)
+    fetch.wait()
     for k in range(2):
 
         def block(i, _, k=k):
@@ -472,7 +516,6 @@
             return 0
 
         lax.fori_loop(0, hidden // wide, block, 0)
-    for k in range(2):
         q_all[mx, k] = jnp.sum(acc[k].T, axis=0, keepdims=True)
 
     def q_copy(o):
@@ -481,116 +524,126 @@
 
     for o in range(1, nx):
         q_copy(o).start()
+
+    half = nz // 2
+    arrivals = [0] + [o % nz for k in range(1, half) for o in (k, -k)] + [half]
+
+    def x_copy(o):
+        ref = rows.at[c, hh, zo(-o)]
+        return remote(ref, ref, x_sems.at[0, o], x_sems.at[1, o], {"member": neighbor})
+
+    def pair_copy(part, o):
+        ref = rows.at[c, hh + part - 2 * hh * part, zo(-o)]
+        return remote(ref, ref, pair_sems.at[0, part, o], pair_sems.at[1, part, o], {"dp": partner})
+
+    def arrive(o):
+        ref = rows.at[c, hh, zo(-o)]
+        if o == 0:
+            ref = rows.at[c, hh, z, pl.ds(0, flat - 1)]
+        remote(ref, ref, row_send, row_recv.at[o], {"dp": partner}).wait_recv()
+        x_copy(o).start()
+        pair_copy(0, o).start()
+
+    shift_out[...] = critic_shift[pl.ds(c, 1), :]
+    head_out[...] = critic_head[pl.ds(c, 1), :]
+    fetch_critic.wait()
+    critic_out[...] = critic_w1[...].astype(bf16)
+    early = nz // 2
+    for o in arrivals[:early]:
+        arrive(o)
+
     for o in range(1, nx):
         q_copy(o).wait_recv()
     first = jnp.zeros((1, tokens), f32)
     second = first
     for k in range(2 * nx):
         value = q_all[k // 2, k % 2]
-        first = jnp.where(ints[2:3, :] == k, value, first)
-        second = jnp.where(ints[3:4, :] == k, value, second)
+        first = jnp.where(subset[0:1, :] == k, value, first)
+        second = jnp.where(subset[1:2, :] == k, value, second)
     lowest = jnp.minimum(first, second)
-    carry = 1.0 - ints[0:1, :].astype(f32)
-    target = reals[0:1, :] + GAMMA * carry * (lowest - ALPHA * reals[1:2, :])
+    carry = 1.0 - terminal[...].astype(f32)
+    target = as_row(rewards) + GAMMA * carry * (lowest - ALPHA * as_row(next_logp))
 
     lane = iota((128, tokens), 0)
     spread = jnp.where(to_shard, target, 0.0).astype(bf16)
     spread_w = jnp.where(to_shard, weight, 0.0).astype(bf16)
-    note = dot_nt(spread, ones_where(lane == rank)) + dot_nt(
-        spread_w, ones_where(lane == rank + cap)
-    )
+    note = dot_nt(spread, ones_where(lane == rank)) + dot_nt(spread_w, ones_where(lane == rank + cap))
     sent_notes[...] = note.reshape(shards, 1, 128)
-
-    def note_copy(i):
-        to = peer(i, 1)
-        return remote(
-            sent_notes.at[to],
-            notes.at[lax.rem(to, 2), me],
-            note_sems.at[0, i],
-            note_sems.at[1, i],
-            {"dp": to},
-        )
-
-    def note_landed(i):
-        ref = notes.at[c, peer(i, -1)]
-        return remote(ref, ref, note_sems.at[0, i], note_sems.at[1, i], {"dp": peer(i, 1)})
-
-    def send_notes(i, _):
-        note_copy(step_of(i)).start()
-        return 0
-
-    lax.fori_loop(0, shards - 1, send_notes, 0)
-    notes[c, me] = sent_notes[me]
-
-    def pair_copy(i):
-        ref = rows.at[c, peer(i, -1)]
-        return remote(ref, ref, pair_sems.at[0, i], pair_sems.at[1, i], {"dp": partner})
-
-    pair_copy(last).start()
-
-    def relay(i, _):
-        step = step_of(shards - 2 - i)
-        row_landed(step).wait_recv()
-        pair_copy(step).start()
-        return 0
-
-    lax.fori_loop(0, shards - 1, relay, 0)
-
-    def note_wait(i, _):
-        note_landed(step_of(i)).wait_recv()
-        return 0
-
-    lax.fori_loop(0, shards - 1, note_wait, 0)
+    mine = z * flat + y * 2 + c
+
+    def send_notes(oz, to, place, cc):
+        remote(
+            sent_notes.at[place], notes.at[cc, mine], note_sems.at[0], note_sems.at[1], {"dp": to}
+        ).start()
+
+    each(send_notes)
+    notes[c, mine] = sent_notes[mine]
+
+    for o in arrivals[early:]:
+        arrive(o)
+    for o in arrivals:
+        x_copy(o).wait_recv()
+        pair_copy(1, o).start()
+    most = notes.at[c, pl.ds(0, shards - 1)]
+    all_notes = remote(most, most, note_sems.at[0], note_sems.at[1], {"dp": partner})
+    all_notes.wait_recv()
     pair_n = remote(notes.at[c], notes.at[c], pair_note.at[0], pair_note.at[1], {"dp": partner})
     pair_n.start()
 
-    def drain(i, _):
-        row_copy(step_of(i)).wait_send()
-        note_copy(step_of(i)).wait_send()
-        return 0
-
-    lax.fori_loop(0, shards - 1, drain, 0)
-
-    def pair_wait(i, _):
-        pair_copy(i).wait()
-        return 0
-
-    lax.fori_loop(0, shards, pair_wait, 0)
+    all_notes.wait_send()
+    most = sent.at[pl.ds(0, shards - 1)]
+    remote(most, most, row_send, row_recv.at[0], {"dp": partner}).wait_send()
     for o in range(1, nx):
         q_copy(o).wait_send()
+    for o in arrivals:
+        x_copy(o).wait_send()
+        pair_copy(0, o).wait()
+        pair_copy(1, o).wait()
     pair_n.wait()
 
 
-def dispatch(features, next_features, ints, reals, source_weight, targets, ny, nz, nx):
+def dispatch(features, next_features, small, targets, critics, ny, nz, nx):
     tokens, width = features.shape
     shards = 2 * ny * nz
     cap = 2 * tokens // shards
     f32, bf16 = jnp.float32, jnp.bfloat16
     vmem = pl.BlockSpec(memory_space=pltpu.VMEM)
     dma = pltpu.SemaphoreType.DMA
+    w1 = targets[0]
     return pl.pallas_call(
         functools.partial(dispatch_kernel, ny, nz, nx, cap),
         out_shape=(
-            jax.ShapeDtypeStruct((2, shards, cap, width), bf16),
-            jax.ShapeDtypeStruct((2, shards, 1, 128), f32),
+            pltpu.VMEM((2, 2, nz, 2 * ny, cap // 2, width), bf16),
+            pltpu.VMEM((2, shards, 1, 128), f32),
+            pltpu.VMEM((1, w1.shape[1]), f32),
+            pltpu.VMEM((1, w1.shape[1]), f32),
+            pltpu.VMEM(w1.shape[1:], bf16),
         ),
-        in_specs=[vmem] * 4 + [pl.BlockSpec(memory_space=pltpu.SMEM)] + [vmem] * 5,
-        out_specs=[vmem] * 2,
+        in_specs=[vmem] * 15 + [pl.BlockSpec(memory_space=pltpu.HBM)] * 2,
+        out_specs=[vmem] * 5,
         scratch_shapes=[
-            pltpu.VMEM((shards, cap, width), bf16),
+            pltpu.VMEM(w1.shape, w1.dtype),
+            pltpu.VMEM(w1.shape[1:], f32),
+            pltpu.VMEM((shards, cap // 2, width), bf16),
             pltpu.VMEM((shards, 1, 128), f32),
             pltpu.VMEM((nx, 2, 1, tokens), f32),
             pltpu.VMEM((2, tokens, 128), f32),
-            dma((2, shards)),
-            dma((2, shards)),
-            dma((2, shards)),
+            dma,
+            dma,
+            dma,
+            dma((nz,)),
+            dma((2,)),
+            dma((2, nz)),
+            dma((2, 2, nz)),
             dma((2,)),
             dma((2, nx - 1)),
         ],
-        compiler_params=pltpu.CompilerParams(collective_id=1, has_side_effects=True),
+        compiler_params=pltpu.CompilerParams(
+            collective_id=1, has_side_effects=True, vmem_limit_bytes=56 * 2**20
+        ),
         cost_estimate=pl.CostEstimate(flops=10**9, bytes_accessed=4 * 10**6, transcendentals=0),
         name="dispatch",
-    )(features, next_features, ints, reals, source_weight, *targets)
+    )(features, next_features, *small, *critics[1:], *targets[1:], w1, critics[0])
 
 
 def critic_kernel(
@@ -598,13 +651,11 @@
     tile,
     rows,
     notes,
-    shift_all,
-    head_all,
-    w_hbm,
+    shift_ref,
+    head_ref,
+    w,
     h,
     hs,
-    w_wide,
-    w,
     xc,
     targets,
     weights,
@@ -615,7 +666,6 @@
     sq,
     s0,
     s1,
-    sem,
 ):
     f32, bf16 = jnp.float32, jnp.bfloat16
     slots, width = rows.shape[1:]
@@ -625,14 +675,13 @@
     few, many = 3, 6
     wide = min(256, hidden)
     lanes = hidden // 128
-    c = lax.rem(lax.axis_index("dp"), 2)
-    fetch = pltpu.make_async_copy(w_hbm.at[c], w_wide, sem)
-    fetch.start()
-    shift = shift_all[pl.ds(c, 1), :]
-    head = head_all[pl.ds(c, 1), :]
-
-    owner = ones_where(iota((shards, slots), 1) // cap == iota((shards, slots), 0))
-    my_slot = lax.rem(iota((cap, slots), 1), cap) == iota((cap, slots), 0)
+    shift = shift_ref[...]
+    head = head_ref[...]
+
+    kept, part = cap // 2, slots // 2
+    at_slot = iota((1, slots), 1)
+    owner = ones_where(lax.rem(at_slot, part) // kept == iota((shards, slots), 0))
+    my_slot = at_slot // part * kept + lax.rem(at_slot, kept) == iota((cap, slots), 0)
     upto = ones_where(iota((128, 128), 0) <= iota((128, 128), 1))
     counts = []
     for s in range(2):
@@ -671,8 +720,6 @@
 
         lax.fori_loop(0, trips, compact, 0)
 
-    fetch.wait()
-    w[...] = w_wide[...].astype(bf16)
     total0 = jnp.zeros((1, hidden), f32)
     total1 = jnp.zeros((1, hidden), f32)
     groups = tile // 8
@@ -777,7 +824,7 @@
 def critic_sums(rows, notes, shift, head, w1, cap):
     f32, bf16 = jnp.float32, jnp.bfloat16
     slots, width = rows.shape[1:]
-    hidden = w1.shape[1]
+    hidden = w1.shape[0]
     tile = slots * 3 // 16
     tall = 6 * tile
     vmem = pl.BlockSpec(memory_space=pltpu.VMEM)
@@ -785,14 +832,12 @@
     return pl.pallas_call(
         functools.partial(critic_kernel, cap, tile),
         out_shape=(
-            jax.ShapeDtypeStruct((blocks, 128, 128), bf16),
-            jax.ShapeDtypeStruct((blocks, 1, 128), f32),
+            pltpu.VMEM((blocks, 128, 128), bf16),
+            pltpu.VMEM((blocks, 1, 128), f32),
         ),
-        in_specs=[vmem] * 4 + [pl.BlockSpec(memory_space=pl.ANY)],
+        in_specs=[vmem] * 5,
         out_specs=[vmem] * 2,
         scratch_shapes=[
-            pltpu.VMEM((hidden, width), f32),
-            pltpu.VMEM((hidden, width), bf16),
             pltpu.VMEM((2, tall, width), bf16),
             pltpu.VMEM((2, tall, 128), f32),
             pltpu.VMEM((2, tall, 128), f32),
@@ -803,9 +848,8 @@
             pltpu.VMEM((8, hidden), f32),
             pltpu.VMEM((8, hidden), f32),
             pltpu.VMEM((8, hidden), f32),
-            pltpu.SemaphoreType.DMA,
         ],
-        compiler_params=pltpu.CompilerParams(vmem_limit_bytes=60 * 2**20),
+        compiler_params=pltpu.CompilerParams(vmem_limit_bytes=48 * 2**20),
         cost_estimate=pl.CostEstimate(
             flops=8 * slots * hidden * width, bytes_accessed=4 * 10**6, transcendentals=0
         ),
@@ -840,36 +884,31 @@
     tokens, width = features.shape
     critics, hidden = critic_w1.shape[:2]
     cap = 2 * tokens // shards
-    zero = jnp.zeros_like(terminal)
-    ints = jnp.stack(
-        [terminal, source_ids, subset[:, 0], subset[:, 1], destination, zero, zero, zero]
-    )
-    reals = jnp.stack([rewards, next_logp]).astype(f32)
-    rows, notes = dispatch(
+    rows, notes, shift, head, w1 = dispatch(
         features,
         next_features,
-        ints,
-        reals,
-        source_weight.astype(f32),
+        (
+            destination.reshape(1, tokens),
+            terminal.reshape(1, tokens),
+            source_ids.reshape(1, tokens),
+            subset.T,
+            rewards.reshape(tokens // 128, 128),
+            next_logp.reshape(tokens // 128, 128),
+            source_weight.reshape(1, -1),
+        ),
         (target_w1, target_mean, target_scale, target_shift, target_head),
+        (critic_w1, critic_shift, critic_head),
         ny,
         nz,
         nx,
     )
-    h, hs = critic_sums(
-        rows.reshape(2, shards * cap, width), notes, critic_shift, critic_head, critic_w1, cap
-    )
+    h, hs = critic_sums(rows.reshape(2, shards * cap, width), notes, shift, head, w1, cap)
     h = h.reshape(ny, nz, 128, 128)
     hs = hs.reshape(ny, nz, 1, 128)
-    full, small, squares = reduce_all(h, hs, ny, nz, nx)
-    root = jnp.float32(math.sqrt(critics * nx * hidden * (width + 2)))
-    norm = jnp.sqrt(squares[0, 0])
-    factor = root / jnp.maximum(norm, root)
+    full, shift, head, factor = reduce_all(h, hs, ny, nz, nx)
+    factor = factor[0, 0]
     step_w1 = full.reshape(critics, hidden, width).astype(f32) * factor
-    small = small[..., 0, 0:128].reshape(critics, hidden // 128, 2, 128)
-    step_shift = small[:, :, 0, :].reshape(critics, hidden) * factor
-    step_head = small[:, :, 1, :].reshape(critics, hidden) * factor
-    return (step_w1, step_shift, step_head)
+    return (step_w1, shift * factor, head * factor)
 
 
 def solution(mesh):

time: 117 us -> 92.2 us (0.79)
  Pallas kernels: 105 us -> 88.2 us
  local copies, waits for them, and re-layouts: 4.86 us -> 0 us
  other arithmetic: 5.99 us -> 3.23 us
    pallas_call x1, Pallas kernels: 38 us -> 29.2 us  [dispatch(): pl.pallas_call(functools.partial(dispatch_kernel, ny, nz, nx, cap), out_s...]
    pallas_call x2, Pallas kernels: 66.6 us -> 59 us  [the longest x1 42.3 us: reduce_all(): pl.pallas_call(functools.partial(reduce_kernel, ny, nz, nx), out_shape=(p...]
    another operation x6 -> x0, local copies, waits for them, and re-layouts: 3.48 us -> none  [the longest x4 2.11 us: per_device(): jnp.stack([terminal, source_ids, subset[:, 0], subset[:, 1], destination,...]
    convert_element_type x2 -> x0, other arithmetic: 1.77 us -> none  [the longest x1 1.17 us: per_device(): source_weight.astype(f32)]
    mul x1, other arithmetic: 4.13 us -> 2.58 us  [per_device(): step_w1 = full.reshape(critics, hidden, width).astype(f32) * factor]
where the time goes in v4:
time: 92.2 us; the launch traced here: 92.1 us
  Pallas kernels  88.2 us (96%)
  other arithmetic  3.23 us (4%)
    pallas_call x1, Pallas kernels, reduce_all(): pl.pallas_call(functools.partial(reduce_kernel, ny, nz, nx), out_shape=(p...  42.3 us
    pallas_call x1, Pallas kernels, dispatch(): pl.pallas_call(functools.partial(dispatch_kernel, ny, nz, nx, cap), out_s...  29.2 us
    pallas_call x1, Pallas kernels, critic_sums(): pl.pallas_call(functools.partial(critic_kernel, cap, tile), out_shape=(pl...  16.7 us
    mul x1, other arithmetic, per_device(): step_w1 = full.reshape(critics, hidden, width).astype(f32) * factor  2.58 us

profile of v4, /device:TPU:1, one launch (start us, length us, event | category | flops | bytes accessed | tf_op | source)
XLA Modules:
  0.0 92.1 jit_solution(2387217550930075172)
XLA Ops:
  0.6 29.2 %dispatch.1 = (bf16[2,2,8,8,8,256]{5,4,3,2,1,0:T(8,128)(2,1)S(1)}, f32[2,64,1,128]{3,2,1,0:T(1,128)S(1)}, f32[1,2048]{1,0:T(1,128)S(1)}, f32[1,2048]{1,0:T(1,128)S(1)}, bf16[2048,256]{1,0:T(8,128)(2,1)S(1)}) custom-call(bf16[512,256]{1,0:T(8,128)(2,1)} %features.1, bf16[512,256]{1,0:T(8,128)(2,1)} %next_features.1, s32[1,512]{1,0:T(1,128)} %bitcast.20, ...), custom_call_target="tpu_custom_call" | custom-call | flops 1000000000 | bytes 4000000 | tf_op jit(solution)/shard_map/dispatch/pallas_call | solution.py:613
  29.9 16.7 %critic_sums.1 = (bf16[32,128,128]{2,1,0:T(8,128)(2,1)S(1)}, f32[32,1,128]{2,1,0:T(1,128)S(1)}) custom-call(bf16[2,1024,256]{2,1,0:T(8,128)(2,1)S(1)} %bitcast.17, f32[2,64,1,128]{3,2,1,0:T(1,128)S(1)} %get-tuple-element.15.notes, f32[1,2048]{1,0:T(1,128)S(1)} %get-tuple-element.16.shift_ref, f32[1,2048]{1,0:T(1,128)S(1)} %get-tuple-element.17.head_ref, ...), custom_call_target="tpu_custom_call" | custom-call | flops 4294967296 | bytes 4000000 | tf_op jit(solution)/shard_map/critic_sums/pallas_call | solution.py:832
  46.5 42.3 %gradient_sum.1 = (bf16[2,16,128,256]{3,2,1,0:T(8,128)(2,1)S(1)}, f32[2,2048]{1,0:T(2,128)S(1)}, f32[2,2048]{1,0:T(2,128)S(1)}, f32[1,128]{1,0:T(1,128)S(1)}) custom-call(bf16[4,8,128,128]{3,2,1,0:T(8,128)(2,1)S(1)} %bitcast.13, f32[4,8,1,128]{3,2,1,0:T(1,128)S(1)} %bitcast.14), custom_call_target="tpu_custom_call" | custom-call | flops 10000000 | bytes 4000000 | tf_op jit(solution)/shard_map/gradient_sum/pallas_call | solution.py:299
  88.9 0.7 broadcast_multiply_fusion
  89.5 2.6 %convert_multiply_fusion = f32[2,16,128,256]{3,2,1,0:T(8,128)} fusion(bf16[2,16,128,256]{3,2,1,0:T(8,128)(2,1)S(1)} %get-tuple-element.21, f32[]{:T(128)S(1)} %bitcast.16), kind=kLoop, calls=%fused_computation | loop fusion | flops 2097152 | bytes 6291460 | tf_op jit(solution)/shard_map/mul | solution.py:910

commit v5 on v4

--- a/solution.py
+++ b/solution.py
@@ -440,12 +440,13 @@
             act(oz, (yy * nz + zz) * 2 + cc, zz * flat + yy * 2 + cc, cc)
 
     def each(act):
+        group(0, True, act)
+
         def step(i, _):
-            group(far_first(i, nz), False, act)
+            group(near_first(i, nz), False, act)
             return 0
 
         lax.fori_loop(0, nz - 1, step, 0)
-        group(0, True, act)
 
     barrier = pltpu.get_barrier_semaphore()
 
@@ -495,7 +496,7 @@
 
     hidden = target_w1.shape[1]
     wide = min(256, hidden)
-    tall = min(128, tokens)
+    tall = min(512, tokens)
     acc[...] = jnp.zeros(acc.shape, f32)
     fetch.wait()
     for k in range(2):
@@ -547,7 +548,10 @@
     shift_out[...] = critic_shift[pl.ds(c, 1), :]
     head_out[...] = critic_head[pl.ds(c, 1), :]
     fetch_critic.wait()
-    critic_out[...] = critic_w1[...].astype(bf16)
+    step = min(256, critic_w1.shape[0])
+    for i in range(critic_w1.shape[0] // step):
+        cut = slice(i * step, (i + 1) * step)
+        critic_out[:, cut] = critic_w1[cut, :].T.astype(bf16)
     early = nz // 2
     for o in arrivals[:early]:
         arrive(o)
@@ -617,7 +621,7 @@
             pltpu.VMEM((2, shards, 1, 128), f32),
             pltpu.VMEM((1, w1.shape[1]), f32),
             pltpu.VMEM((1, w1.shape[1]), f32),
-            pltpu.VMEM(w1.shape[1:], bf16),
+            pltpu.VMEM(w1.shape[:0:-1], bf16),
         ),
         in_specs=[vmem] * 15 + [pl.BlockSpec(memory_space=pltpu.HBM)] * 2,
         out_specs=[vmem] * 5,
@@ -661,7 +665,6 @@
     weights,
     zbuf,
     gbuf,
-    gz,
     gt,
     sq,
     s0,
@@ -669,10 +672,11 @@
 ):
     f32, bf16 = jnp.float32, jnp.bfloat16
     slots, width = rows.shape[1:]
-    hidden = w.shape[0]
+    hidden = w.shape[1]
     shards = slots // cap
     pieces = slots // 128
     few, many = 3, 6
+    big = few * tile
     wide = min(256, hidden)
     lanes = hidden // 128
     shift = shift_ref[...]
@@ -705,20 +709,22 @@
             start = start + running[p : p + 1, 127:128]
         number = jnp.sum(alive)
         counts.append(number)
-        y_wide = jnp.broadcast_to(y_row, (128, slots)).astype(bf16)
-        w_wide_row = jnp.broadcast_to(w_row, (128, slots)).astype(bf16)
+        yw = jnp.concatenate(
+            [jnp.broadcast_to(y_row, (128, slots)), jnp.broadcast_to(w_row, (128, slots))], axis=0
+        ).astype(bf16)
         trips = jnp.where(number <= few * tile, few, many)
 
-        def compact(i, _, s=s, place=place, y_wide=y_wide, w_wide_row=w_wide_row):
-            at = pl.ds(pl.multiple_of(i * tile, tile), tile)
-            row = iota((tile, 128), 0) + i * tile
+        def compact(i, _, s=s, place=place, yw=yw):
+            at = pl.ds(pl.multiple_of(i * big, big), big)
+            row = iota((big, 128), 0) + i * big
             pick = jnp.concatenate([ones_where(row == p) for p in place], axis=1)
             xc[s, at, :] = dot_nn(pick, rows[s]).astype(bf16)
-            targets[s, at, :] = dot_nt(pick, y_wide)
-            weights[s, at, :] = dot_nt(pick, w_wide_row)
+            both = dot_nt(pick, yw)
+            targets[s, at, :] = both[:, 0:128]
+            weights[s, at, :] = both[:, 128:256]
             return 0
 
-        lax.fori_loop(0, trips, compact, 0)
+        lax.fori_loop(0, trips // few, compact, 0)
 
     total0 = jnp.zeros((1, hidden), f32)
     total1 = jnp.zeros((1, hidden), f32)
@@ -735,7 +741,7 @@
         parts = jnp.concatenate(
             [one.astype(f32), two.astype(f32), three.astype(f32), jnp.zeros((13, width), f32)], axis=0
         ).astype(bf16)
-        mu = jnp.sum(dot_nt(parts, w[...]), axis=0, keepdims=True)
+        mu = jnp.sum(dot_nn(parts, w[...]), axis=0, keepdims=True)
         sq[...] = jnp.zeros(sq.shape, f32)
         s0[...] = jnp.zeros(s0.shape, f32)
         s1[...] = jnp.zeros(s1.shape, f32)
@@ -746,7 +752,7 @@
             alive = jnp.where(row < number.astype(jnp.int32), 1.0, 0.0)
             x = xc[s, at, :]
             for j in range(hidden // wide):
-                pre = dot_nt(x, w[j * wide : (j + 1) * wide, :])
+                pre = dot_nn(x, w[:, j * wide : (j + 1) * wide])
                 for k in range(wide // 128):
                     lo = j * wide + k * 128
                     zc = (pre[:, k * 128 : (k + 1) * 128] - mu[:, lo : lo + 128]) * alive
@@ -786,30 +792,31 @@
         base = -scale * (sum0 / whole)
         tilt = -scale * (sum1 / whole)
 
-        def backward(i, _, scale=scale, base=base, tilt=tilt):
-            at = pl.ds(pl.multiple_of(i * tile, tile), tile)
-            for j in range(lanes):
-                cut = slice(j * 128, (j + 1) * 128)
-                value = gbuf[at, cut] * scale[:, cut] + (zbuf[at, cut] * tilt[:, cut] + base[:, cut])
-                gz[at, cut] = value.astype(bf16)
-            return 0
-
-        lax.fori_loop(0, trips, backward, 0)
-
-        def product(depth, s=s):
-            x = xc[s, 0:depth, :]
+        def slope_of(at, cut, scale=scale, base=base, tilt=tilt):
+            value = gbuf[at, cut] * scale[:, cut] + (zbuf[at, cut] * tilt[:, cut] + base[:, cut])
+            return value.astype(bf16)
+
+        @pl.when(trips == few)
+        def _(s=s, slope_of=slope_of):
+            xt = xc[s, 0:big, :].T
             for j in range(hidden // wide):
                 cut = slice(j * wide, (j + 1) * wide)
-                out = dot_tn(x, gz[0:depth, cut])
+                out = dot_nn(xt, slope_of(slice(0, big), cut))
                 gt[:, cut] = out if s == 0 else gt[:, cut] + out
 
-        @pl.when(trips == few)
-        def _():
-            product(few * tile)
-
         @pl.when(trips != few)
-        def _():
-            product(many * tile)
+        def _(s=s, slope_of=slope_of):
+            if s == 0:
+                gt[...] = jnp.zeros(gt.shape, f32)
+
+            def step(i, _):
+                at = pl.ds(pl.multiple_of(i * tile, tile), tile)
+                for j in range(hidden // wide):
+                    cut = slice(j * wide, (j + 1) * wide)
+                    gt[:, cut] += dot_tn(xc[s, at, :], slope_of(at, cut))
+                return 0
+
+            lax.fori_loop(0, many, step, 0)
 
     g_shift = head * total0
     g_head = shift * total0 + total1
@@ -824,7 +831,7 @@
 def critic_sums(rows, notes, shift, head, w1, cap):
     f32, bf16 = jnp.float32, jnp.bfloat16
     slots, width = rows.shape[1:]
-    hidden = w1.shape[0]
+    hidden = w1.shape[1]
     tile = slots * 3 // 16
     tall = 6 * tile
     vmem = pl.BlockSpec(memory_space=pltpu.VMEM)
@@ -843,7 +850,6 @@
             pltpu.VMEM((2, tall, 128), f32),
             pltpu.VMEM((tall, hidden), f32),
             pltpu.VMEM((tall, hidden), f32),
-            pltpu.VMEM((tall, hidden), bf16),
             pltpu.VMEM((width, hidden), f32),
             pltpu.VMEM((8, hidden), f32),
             pltpu.VMEM((8, hidden), f32),

time: 92.2 us -> 88.4 us (0.959)
  Pallas kernels: 88.2 us -> 84.4 us
    pallas_call x1, Pallas kernels: 16.7 us -> 12.5 us  [critic_sums(): pl.pallas_call(functools.partial(critic_kernel, cap, tile), out_shape=(pl...]
where the time goes in v5:
time: 88.4 us; the launch traced here: 88.3 us
  Pallas kernels  84.4 us (95%)
  other arithmetic  3.23 us (4%)
    pallas_call x1, Pallas kernels, reduce_all(): pl.pallas_call(functools.partial(reduce_kernel, ny, nz, nx), out_shape=(p...  42.4 us
    pallas_call x1, Pallas kernels, dispatch(): pl.pallas_call(functools.partial(dispatch_kernel, ny, nz, nx, cap), out_s...  29.5 us
    pallas_call x1, Pallas kernels, critic_sums(): pl.pallas_call(functools.partial(critic_kernel, cap, tile), out_shape=(pl...  12.5 us
    mul x1, other arithmetic, per_device(): step_w1 = full.reshape(critics, hidden, width).astype(f32) * factor  2.58 us

profile of v5, /device:TPU:1, one launch (start us, length us, event | category | flops | bytes accessed | tf_op | source)
XLA Modules:
  0.0 88.3 jit_solution(12639998699738882581)
XLA Ops:
  0.6 29.5 %dispatch.1 = (bf16[2,2,8,8,8,256]{5,4,3,2,1,0:T(8,128)(2,1)S(1)}, f32[2,64,1,128]{3,2,1,0:T(1,128)S(1)}, f32[1,2048]{1,0:T(1,128)S(1)}, f32[1,2048]{1,0:T(1,128)S(1)}, bf16[256,2048]{1,0:T(8,128)(2,1)S(1)}) custom-call(bf16[512,256]{1,0:T(8,128)(2,1)} %features.1, bf16[512,256]{1,0:T(8,128)(2,1)} %next_features.1, s32[1,512]{1,0:T(1,128)} %bitcast.20, ...), custom_call_target="tpu_custom_call" | custom-call | flops 1000000000 | bytes 4000000 | tf_op jit(solution)/shard_map/dispatch/pallas_call | solution.py:617
  30.1 12.5 %critic_sums.1 = (bf16[32,128,128]{2,1,0:T(8,128)(2,1)S(1)}, f32[32,1,128]{2,1,0:T(1,128)S(1)}) custom-call(bf16[2,1024,256]{2,1,0:T(8,128)(2,1)S(1)} %bitcast.17, f32[2,64,1,128]{3,2,1,0:T(1,128)S(1)} %get-tuple-element.15.notes, f32[1,2048]{1,0:T(1,128)S(1)} %get-tuple-element.16.shift_ref, f32[1,2048]{1,0:T(1,128)S(1)} %get-tuple-element.17.head_ref, ...), custom_call_target="tpu_custom_call" | custom-call | flops 4294967296 | bytes 4000000 | tf_op jit(solution)/shard_map/critic_sums/pallas_call | solution.py:839
  42.6 42.4 %gradient_sum.1 = (bf16[2,16,128,256]{3,2,1,0:T(8,128)(2,1)S(1)}, f32[2,2048]{1,0:T(2,128)S(1)}, f32[2,2048]{1,0:T(2,128)S(1)}, f32[1,128]{1,0:T(1,128)S(1)}) custom-call(bf16[4,8,128,128]{3,2,1,0:T(8,128)(2,1)S(1)} %bitcast.13, f32[4,8,1,128]{3,2,1,0:T(1,128)S(1)} %bitcast.14), custom_call_target="tpu_custom_call" | custom-call | flops 10000000 | bytes 4000000 | tf_op jit(solution)/shard_map/gradient_sum/pallas_call | solution.py:299
  85.0 0.7 broadcast_multiply_fusion
  85.7 2.6 %convert_multiply_fusion = f32[2,16,128,256]{3,2,1,0:T(8,128)} fusion(bf16[2,16,128,256]{3,2,1,0:T(8,128)(2,1)S(1)} %get-tuple-element.21, f32[]{:T(128)S(1)} %bitcast.16), kind=kLoop, calls=%fused_computation | loop fusion | flops 2097152 | bytes 6291460 | tf_op jit(solution)/shard_map/mul | solution.py:916

commit v6 on v5

--- a/solution.py
+++ b/solution.py
@@ -516,7 +516,7 @@
                 acc[k, t * tall : (t + 1) * tall, :] += total
             return 0
 
-        lax.fori_loop(0, hidden // wide, block, 0)
+        lax.fori_loop(0, hidden // wide, block, 0, unroll=min(4, hidden // wide))
         q_all[mx, k] = jnp.sum(acc[k].T, axis=0, keepdims=True)
 
     def q_copy(o):

time: 88.4 us -> 86 us (0.973)
  Pallas kernels: 84.4 us -> 82 us
    pallas_call x1, Pallas kernels: 42.4 us -> 40.9 us  [reduce_all(): pl.pallas_call(functools.partial(reduce_kernel, ny, nz, nx), out_shape=(p...]
where the time goes in v6:
time: 86 us; the launch traced here: 85.9 us
  Pallas kernels  82 us (95%)
  other arithmetic  3.23 us (4%)
    pallas_call x1, Pallas kernels, reduce_all(): pl.pallas_call(functools.partial(reduce_kernel, ny, nz, nx), out_shape=(p...  40.9 us
    pallas_call x1, Pallas kernels, dispatch(): pl.pallas_call(functools.partial(dispatch_kernel, ny, nz, nx, cap), out_s...  28.6 us
    pallas_call x1, Pallas kernels, critic_sums(): pl.pallas_call(functools.partial(critic_kernel, cap, tile), out_shape=(pl...  12.5 us
    mul x1, other arithmetic, per_device(): step_w1 = full.reshape(critics, hidden, width).astype(f32) * factor  2.58 us

profile of v6, /device:TPU:1, one launch (start us, length us, event | category | flops | bytes accessed | tf_op | source)
XLA Modules:
  0.0 85.9 jit_solution(16085027897489579918)
XLA Ops:
  0.6 28.6 %dispatch.1 = (bf16[2,2,8,8,8,256]{5,4,3,2,1,0:T(8,128)(2,1)S(1)}, f32[2,64,1,128]{3,2,1,0:T(1,128)S(1)}, f32[1,2048]{1,0:T(1,128)S(1)}, f32[1,2048]{1,0:T(1,128)S(1)}, bf16[256,2048]{1,0:T(8,128)(2,1)S(1)}) custom-call(bf16[512,256]{1,0:T(8,128)(2,1)} %features.1, bf16[512,256]{1,0:T(8,128)(2,1)} %next_features.1, s32[1,512]{1,0:T(1,128)} %bitcast.20, ...), custom_call_target="tpu_custom_call" | custom-call | flops 1000000000 | bytes 4000000 | tf_op jit(solution)/shard_map/dispatch/pallas_call | solution.py:617
  29.2 12.5 %critic_sums.1 = (bf16[32,128,128]{2,1,0:T(8,128)(2,1)S(1)}, f32[32,1,128]{2,1,0:T(1,128)S(1)}) custom-call(bf16[2,1024,256]{2,1,0:T(8,128)(2,1)S(1)} %bitcast.17, f32[2,64,1,128]{3,2,1,0:T(1,128)S(1)} %get-tuple-element.15.notes, f32[1,2048]{1,0:T(1,128)S(1)} %get-tuple-element.16.shift_ref, f32[1,2048]{1,0:T(1,128)S(1)} %get-tuple-element.17.head_ref, ...), custom_call_target="tpu_custom_call" | custom-call | flops 4294967296 | bytes 4000000 | tf_op jit(solution)/shard_map/critic_sums/pallas_call | solution.py:839
  41.7 40.9 %gradient_sum.1 = (bf16[2,16,128,256]{3,2,1,0:T(8,128)(2,1)S(1)}, f32[2,2048]{1,0:T(2,128)S(1)}, f32[2,2048]{1,0:T(2,128)S(1)}, f32[1,128]{1,0:T(1,128)S(1)}) custom-call(bf16[4,8,128,128]{3,2,1,0:T(8,128)(2,1)S(1)} %bitcast.13, f32[4,8,1,128]{3,2,1,0:T(1,128)S(1)} %bitcast.14), custom_call_target="tpu_custom_call" | custom-call | flops 10000000 | bytes 4000000 | tf_op jit(solution)/shard_map/gradient_sum/pallas_call | solution.py:299
  82.7 0.7 broadcast_multiply_fusion
  83.3 2.6 %convert_multiply_fusion = f32[2,16,128,256]{3,2,1,0:T(8,128)} fusion(bf16[2,16,128,256]{3,2,1,0:T(8,128)(2,1)S(1)} %get-tuple-element.21, f32[]{:T(128)S(1)} %bitcast.16), kind=kLoop, calls=%fused_computation | loop fusion | flops 2097152 | bytes 6291460 | tf_op jit(solution)/shard_map/mul | solution.py:916

commit v7 on v6

--- a/solution.py
+++ b/solution.py
@@ -516,7 +516,7 @@
                 acc[k, t * tall : (t + 1) * tall, :] += total
             return 0
 
-        lax.fori_loop(0, hidden // wide, block, 0, unroll=min(4, hidden // wide))
+        lax.fori_loop(0, hidden // wide, block, 0, unroll=min(8, hidden // wide))
         q_all[mx, k] = jnp.sum(acc[k].T, axis=0, keepdims=True)
 
     def q_copy(o):
@@ -764,9 +764,11 @@
         var = jnp.sum(sq[...], axis=0, keepdims=True) / whole
         inv = 1.0 / jnp.sqrt(var + EPS)
 
+        short = tile // 2
+
         def slopes(i, _, s=s, inv=inv):
-            at = pl.ds(pl.multiple_of(i * tile, tile), tile)
-            acc = jnp.zeros((tile, 128), f32)
+            at = pl.ds(pl.multiple_of(i * short, short), short)
+            acc = jnp.zeros((short, 128), f32)
             for j in range(lanes):
                 cut = slice(j * 128, (j + 1) * 128)
                 zh = zbuf[at, cut] * inv[:, cut]
@@ -779,11 +781,11 @@
                 zh = zbuf[at, cut]
                 g = jnp.where(zh > -shift[:, cut], dq, 0.0)
                 gbuf[at, cut] = g
-                s0[:, cut] += jnp.sum(g.reshape(groups, 8, 128), axis=0)
-                s1[:, cut] += jnp.sum((g * zh).reshape(groups, 8, 128), axis=0)
+                s0[:, cut] += jnp.sum(g.reshape(short // 8, 8, 128), axis=0)
+                s1[:, cut] += jnp.sum((g * zh).reshape(short // 8, 8, 128), axis=0)
             return 0
 
-        lax.fori_loop(0, trips, slopes, 0)
+        lax.fori_loop(0, trips * (tile // short), slopes, 0)
         sum0 = jnp.sum(s0[...], axis=0, keepdims=True)
         sum1 = jnp.sum(s1[...], axis=0, keepdims=True)
         total0 = total0 + sum0

time: 86 us -> 85.2 us (level)
  no operation moved by 1% of the time
where the time goes in v7:
time: 85.2 us; the launch traced here: 85.1 us
  Pallas kernels  81.2 us (95%)
  other arithmetic  3.23 us (4%)
    pallas_call x1, Pallas kernels, reduce_all(): pl.pallas_call(functools.partial(reduce_kernel, ny, nz, nx), out_shape=(p...  40.8 us
    pallas_call x1, Pallas kernels, dispatch(): pl.pallas_call(functools.partial(dispatch_kernel, ny, nz, nx, cap), out_s...  28.6 us
    pallas_call x1, Pallas kernels, critic_sums(): pl.pallas_call(functools.partial(critic_kernel, cap, tile), out_shape=(pl...  11.8 us
    mul x1, other arithmetic, per_device(): step_w1 = full.reshape(critics, hidden, width).astype(f32) * factor  2.58 us

profile of v7, /device:TPU:1, one launch (start us, length us, event | category | flops | bytes accessed | tf_op | source)
XLA Modules:
  0.0 85.1 jit_solution(2854620681126133458)
XLA Ops:
  0.6 28.6 %dispatch.1 = (bf16[2,2,8,8,8,256]{5,4,3,2,1,0:T(8,128)(2,1)S(1)}, f32[2,64,1,128]{3,2,1,0:T(1,128)S(1)}, f32[1,2048]{1,0:T(1,128)S(1)}, f32[1,2048]{1,0:T(1,128)S(1)}, bf16[256,2048]{1,0:T(8,128)(2,1)S(1)}) custom-call(bf16[512,256]{1,0:T(8,128)(2,1)} %features.1, bf16[512,256]{1,0:T(8,128)(2,1)} %next_features.1, s32[1,512]{1,0:T(1,128)} %bitcast.20, ...), custom_call_target="tpu_custom_call" | custom-call | flops 1000000000 | bytes 4000000 | tf_op jit(solution)/shard_map/dispatch/pallas_call | solution.py:617
  29.3 11.8 %critic_sums.1 = (bf16[32,128,128]{2,1,0:T(8,128)(2,1)S(1)}, f32[32,1,128]{2,1,0:T(1,128)S(1)}) custom-call(bf16[2,1024,256]{2,1,0:T(8,128)(2,1)S(1)} %bitcast.17, f32[2,64,1,128]{3,2,1,0:T(1,128)S(1)} %get-tuple-element.15.notes, f32[1,2048]{1,0:T(1,128)S(1)} %get-tuple-element.16.shift_ref, f32[1,2048]{1,0:T(1,128)S(1)} %get-tuple-element.17.head_ref, ...), custom_call_target="tpu_custom_call" | custom-call | flops 4294967296 | bytes 4000000 | tf_op jit(solution)/shard_map/critic_sums/pallas_call | solution.py:841
  41.1 40.8 %gradient_sum.1 = (bf16[2,16,128,256]{3,2,1,0:T(8,128)(2,1)S(1)}, f32[2,2048]{1,0:T(2,128)S(1)}, f32[2,2048]{1,0:T(2,128)S(1)}, f32[1,128]{1,0:T(1,128)S(1)}) custom-call(bf16[4,8,128,128]{3,2,1,0:T(8,128)(2,1)S(1)} %bitcast.13, f32[4,8,1,128]{3,2,1,0:T(1,128)S(1)} %bitcast.14), custom_call_target="tpu_custom_call" | custom-call | flops 10000000 | bytes 4000000 | tf_op jit(solution)/shard_map/gradient_sum/pallas_call | solution.py:299
  81.9 0.7 broadcast_multiply_fusion
  82.5 2.6 %convert_multiply_fusion = f32[2,16,128,256]{3,2,1,0:T(8,128)} fusion(bf16[2,16,128,256]{3,2,1,0:T(8,128)(2,1)S(1)} %get-tuple-element.21, f32[]{:T(128)S(1)} %bitcast.16), kind=kLoop, calls=%fused_computation | loop fusion | flops 2097152 | bytes 6291460 | tf_op jit(solution)/shard_map/mul | solution.py:918
